TPU v7x, 256 devices: a whole 4x4x8 slice. The times are simulated.
256 devices in a mesh: dp: 64 (over y, x, z_lo, core), seq: 4 (over z_hi).
Axes of the slice: x: 4, y: 4, z: 8 (z_hi: 4, z_lo: 2; z = z_hi * 2 + z_lo), core: 2. Of those that a mesh axis runs over, the one named last changes fastest.
Arguments:
- latents: bfloat16 [64, 512, 1536], P('dp', 'seq'), may hold values from -6 to 6
- fresh_noise: bfloat16 [64, 512, 1536], P('dp', 'seq'), may hold values from -6 to 6
- cache_key: bfloat16 [64, 1024, 1536], P('dp', 'seq'), may hold values from -200 to 200, as said below
- cache_value: bfloat16 [64, 1024, 1536], P('dp', 'seq'), may hold values from -6 to 6
- cache_frame: int32 [64, 1024], P('dp', 'seq'), may hold values from 0 to 11
- block_index: int32 [1], replicated, may hold values from 2 to 4
- timestep: int32 [64], P('dp'), may hold values from 20 to 979
- gain_gen: float32 [1536], replicated, may hold values from 0.25 to 1.75
- w_qkv: bfloat16 [1536, 4608], P(None, 'seq'), may hold values from -0.15625 to 0.15625
- w_out: bfloat16 [1536, 1536], P('seq'), may hold values from -0.5 to 0.5
- gain_real: float32 [1536], replicated, may hold values from 0.25 to 1.75
- w_real: bfloat16 [1536, 1536], P(None, 'seq'), may hold values from -0.15625 to 0.15625
- gain_fake: float32 [1536], replicated, may hold values from 0.25 to 1.75
- w_fake: bfloat16 [1536, 1536], P(None, 'seq'), may hold values from -0.15625 to 0.15625
Outputs:
- clean_block: bfloat16 [64, 512, 1536], P('dp', 'seq')
- grad_qkv: float32 [1536, 4608], P('dp', 'seq')
- grad_out: float32 [1536, 1536], P('seq', 'dp')
Inputs may be any that keep to these rules, and one draw needn't show every extreme that they name: `cache_key`: cache keys are finite.
All inputs are finite; a program needn't handle non-finite values. Where the computation divides by a largest or mean magnitude, that divisor is 1e-20 or more.
Results may differ from a plain program's by a relative error of at most 0.02.
The roundings to bfloat16 on the way count: a program that leaves them out, or rounds other values in their place, can miss the bound.
Values may be sent and summed in bfloat16 or wider, within the bound.
No kernel may reach another device: no remote copies, remote signals or barrier semaphores. Data moves between devices by JAX's collectives and lax.ppermute only.
A program may use at most 128 MiB of HBM per device.

v0:
```python
import math

import jax
import jax.numpy as jnp
import numpy as np
from jax import lax
from jax.experimental import pallas as pl
from jax.experimental.pallas import tpu as pltpu
from jax.sharding import PartitionSpec as P


HEAD_DIM = 128
FRAMES = 3
WINDOW_FRAMES = 6
SEQ = 4
PARTS = 64


def shifted(x, by):
    return lax.ppermute(x, "seq", [(i, (i + by) % SEQ) for i in range(SEQ)])


def plane_groups():
    index = np.arange(64).reshape(4, 4, 2, 2)
    return index.transpose(2, 0, 1, 3).reshape(2, 32).tolist()


def chip_groups():
    return np.arange(PARTS).reshape(-1, 2).T.tolist()


def block_of(x, block, axis):
    width = x.shape[axis] // SEQ
    return lax.dynamic_slice_in_dim(x, (block % SEQ) * width, width, axis)


def dot(a, b, contract=((1,), (0,))):
    return lax.dot_general(a, b, (contract, ((), ())), preferred_element_type=jnp.float32)


NT = ((1,), (1,))
TN = ((0,), (0,))
VMEM = pl.BlockSpec(memory_space=pltpu.VMEM)
SMEM = pl.BlockSpec(memory_space=pltpu.SMEM)
ANY = pl.BlockSpec(memory_space=pl.ANY)


def near(*arrays):
    return [pltpu.with_memory_space_constraint(a, pltpu.VMEM) for a in arrays]


def far(*arrays):
    return [pltpu.with_memory_space_constraint(a, pltpu.HBM) for a in arrays]


def far_out(shape):
    return pltpu.HBM(shape, jnp.bfloat16)


def near_out(shape):
    return pltpu.VMEM(shape, jnp.bfloat16)


def within(mebibytes):
    return pltpu.CompilerParams(vmem_limit_bytes=mebibytes * 1024 * 1024)


def place_in_seq(k):
    return lax.rem(lax.axis_index("seq") + k, SEQ)


def normed_rows(values, gain):
    floats = values.astype(jnp.float32)
    return floats * lax.rsqrt(jnp.mean(floats * floats, axis=-1, keepdims=True) + 1e-06) * gain


def slices_kernel(at_ref, a_ref, b_ref, c_ref, o_ref):
    o_ref[0] = a_ref[...]
    o_ref[1] = b_ref[...]
    o_ref[2] = c_ref[...]


def weight_slices(a, b, c, at, rows):
    spec = pl.BlockSpec((rows, a.shape[1]), lambda i, at: (at[0], 0))
    return pl.pallas_call(
        slices_kernel,
        grid_spec=pltpu.PrefetchScalarGridSpec(
            num_scalar_prefetch=1,
            grid=(1,),
            in_specs=[spec] * 3,
            out_specs=pl.BlockSpec((3, rows, a.shape[1]), lambda i, at: (0, 0, 0)),
        ),
        out_shape=far_out((3, rows, a.shape[1])),
        name="weight_slices",
    )(at, *far(a, b, c))


def place_kernel(*refs):
    o_ref = refs[-1]
    width = refs[0].shape[2]
    for k in range(SEQ):
        lead = pl.multiple_of(place_in_seq(k) * width, 128)
        o_ref[:, :, pl.ds(lead, width)] = refs[k][...]


def placed(parts):
    n, rows, width = parts[0].shape
    return pl.pallas_call(
        place_kernel,
        in_specs=[VMEM] * SEQ,
        out_specs=VMEM,
        out_shape=far_out((n, rows, width * SEQ)),
        compiler_params=within(4),
        name="placed",
    )(*far(*parts))


def project_kernel(*refs):
    parts, (gain_ref, w_ref, turned_ref, packed_ref, held) = refs[:-5], refs[-5:]
    row = 0
    for part in parts:
        at = slice(row, row + part.shape[0])
        row += part.shape[0]
        held[at] = normed_rows(part[...], gain_ref[...]).astype(jnp.bfloat16)
    count = parts[0].shape[0]
    for k in range(SEQ):
        at = slice(k * count, (k + 1) * count)
        turned_ref[:, at] = held[at].T
    packed_ref[...] = dot(held[...], w_ref[...]).astype(jnp.bfloat16)


def project(parts, gain, w):
    length = parts[0].shape[0] * SEQ
    return pl.pallas_call(
        project_kernel,
        in_specs=[VMEM] * (len(parts) + 2),
        out_specs=[VMEM] * 2,
        out_shape=[near_out((w.shape[0], length)), near_out((length, w.shape[1]))],
        scratch_shapes=[pltpu.VMEM((length, w.shape[0]), jnp.bfloat16)],
        compiler_params=within(24),
        name="project",
    )(*far(parts[0]), *far(*parts[1:]), *far(gain.reshape(1, -1), w))


def weights_kernel(*refs):
    parts, (q_ref, k_ref, o_ref) = refs[:SEQ], refs[SEQ:]
    factor = 1.0 / math.sqrt(HEAD_DIM)
    slots = parts[0].shape[0] - 8
    span = slots * SEQ
    keys = [p[:slots] for p in parts] + [k_ref[...]]
    flags = [
        jnp.concatenate([p[slots + r : slots + r + 1] for r in range(slots // HEAD_DIM)], axis=1)
        > 0.5
        for p in parts
    ]
    step = 128
    for r in range(q_ref.shape[0] // step):
        rows = slice(r * step, (r + 1) * step)
        query = q_ref[rows]
        scores = [dot(query, k, NT) * factor for k in keys]
        for n in range(SEQ):
            scores[n] = jnp.where(flags[n], scores[n], -1e30)
        top = jnp.max(scores[SEQ], axis=-1, keepdims=True)
        for n in range(SEQ):
            top = jnp.maximum(top, jnp.max(scores[n], axis=-1, keepdims=True))
        expo = [jnp.exp(s - top) for s in scores]
        total = sum(jnp.sum(e, axis=-1, keepdims=True) for e in expo)
        over = 1.0 / total
        for n in range(SEQ):
            o_ref[0, rows, n * slots : (n + 1) * slots] = (expo[n] * over).astype(jnp.bfloat16)
        o_ref[0, rows, span:] = (expo[SEQ] * over).astype(jnp.bfloat16)


def attention_weights(key_parts, packed):
    length = packed.shape[0]
    heads = key_parts[0].shape[1] // HEAD_DIM
    rows = key_parts[0].shape[0]
    total = (rows - 8) * SEQ + length
    part = pl.BlockSpec((rows, HEAD_DIM), lambda h: (0, h))
    return pl.pallas_call(
        weights_kernel,
        grid=(heads,),
        in_specs=[part] * SEQ
        + [pl.BlockSpec((length, HEAD_DIM), lambda h, j=j: (0, 3 * h + j)) for j in range(2)],
        out_specs=pl.BlockSpec((1, length, total), lambda h: (h, 0, 0)),
        out_shape=near_out((heads, length, total)),
        compiler_params=within(20),
        name="attention_weights",
    )(*far(*key_parts), *near(packed, packed))


def mix_kernel(*refs):
    w_ref, parts, v_ref, outs = refs[0], refs[1 : SEQ + 1], refs[SEQ + 1], refs[SEQ + 2 :]
    slots = parts[0].shape[0]
    count = outs[0].shape[0]
    mixed = dot(w_ref[0, :, slots * SEQ :], v_ref[...])
    for n in range(SEQ):
        mixed += dot(w_ref[0, :, n * slots : (n + 1) * slots], parts[n][...])
    mixed = mixed.astype(jnp.bfloat16)
    for n in range(SEQ):
        outs[n][...] = mixed[n * count : (n + 1) * count]


def attention_mix(weights, value_parts, packed):
    heads, length, total = weights.shape
    slots, features = value_parts[0].shape
    count = length // SEQ
    return pl.pallas_call(
        mix_kernel,
        grid=(heads,),
        in_specs=[pl.BlockSpec((1, length, total), lambda h: (h, 0, 0))]
        + [pl.BlockSpec((slots, HEAD_DIM), lambda h: (0, h))] * SEQ
        + [pl.BlockSpec((length, HEAD_DIM), lambda h: (0, 3 * h + 2))],
        out_specs=[pl.BlockSpec((count, HEAD_DIM), lambda h: (0, h))] * SEQ,
        out_shape=[far_out((count, features))] * SEQ,
        compiler_params=within(12),
        name="attention_mix",
    )(*near(weights), *far(*value_parts), *near(packed))


def in_terms(total, shape):
    row = lax.broadcasted_iota(jnp.int32, shape, 0)
    result = jnp.zeros(shape, jnp.float32)
    for n in range(3):
        term = total.astype(jnp.bfloat16).astype(jnp.float32)
        result = jnp.where(row == n, term, result)
        total = total - term
    return result.astype(jnp.bfloat16)


def unit_of(grads, entries):
    total = sum(g[-8:, :HEAD_DIM].astype(jnp.float32) for g in grads)
    total = jnp.sum(total, axis=0, keepdims=True)[:, :1]
    return 1.0 / (total / entries + 1e-06)


def middle_kernel(*refs):
    parts, refs = refs[:SEQ], refs[SEQ:]
    blend_ref, latents_ref, fresh_ref, real_gain_ref, fake_gain_ref, w_ref = refs[:6]
    clean_ref, gap_ref = refs[6:8]
    outs, (held, sems) = refs[8 : 8 + SEQ], refs[8 + SEQ :]
    copies = [pltpu.make_async_copy(w_ref.at[n], held.at[n], sems.at[n]) for n in range(3)]
    for c in copies:
        c.start()
    width = parts[0].shape[1]

    def block(k):
        lead = pl.multiple_of(place_in_seq(k) * width, 128)
        return held[0, :, pl.ds(lead, width)]

    copies[0].wait()
    update = dot(parts[0][...], block(0), NT)
    for k in range(1, SEQ):
        update += dot(parts[k][...], block(k), NT)
    clean = (latents_ref[...].astype(jnp.float32) + update).astype(jnp.bfloat16)
    clean_ref[...] = clean
    clean_f = clean.astype(jnp.float32)
    noisy = (
        (blend_ref[0:1, 0:1] * clean_f + blend_ref[1:2, 0:1] * fresh_ref[...].astype(jnp.float32))
        .astype(jnp.bfloat16)
        .astype(jnp.float32)
    )
    scaled = noisy * lax.rsqrt(jnp.mean(noisy * noisy, axis=-1, keepdims=True) + 1e-06)
    real_in = (scaled * real_gain_ref[...]).astype(jnp.bfloat16)
    fake_in = (scaled * fake_gain_ref[...]).astype(jnp.bfloat16)
    copies[1].wait()
    pred_real = noisy + dot(real_in, held[1])
    total = jnp.sum(jnp.abs(clean_f - pred_real), axis=(0, 1), keepdims=True)
    copies[2].wait()
    pred_fake = noisy + dot(fake_in, held[2])
    gap = (pred_fake - pred_real).astype(jnp.bfloat16)
    gap_ref[...] = gap
    count = gap.shape[0]
    terms = in_terms(total, (8, width))
    for k in range(SEQ):
        outs[k][:count] = dot(gap, block(k)).astype(jnp.bfloat16)
        outs[k][count:] = terms


def middle(blend, parts, latents, fresh, gain_real, gain_fake, whole):
    count, width = latents.shape
    return pl.pallas_call(
        middle_kernel,
        in_specs=[VMEM] * (SEQ + 5) + [ANY],
        out_specs=[VMEM] * (2 + SEQ),
        out_shape=[far_out((count, width))] * 2
        + [near_out((count + 8, parts[0].shape[1]))] * SEQ,
        scratch_shapes=[pltpu.VMEM(whole.shape, jnp.bfloat16), pltpu.SemaphoreType.DMA((3,))],
        compiler_params=within(30),
        name="middle",
    )(
        *far(*parts, blend, latents, fresh, gain_real.reshape(1, -1), gain_fake.reshape(1, -1)),
        *far(whole),
    )


def split_rows(held, send_ref, keep_ref):
    core = lax.rem(lax.axis_index("dp"), 2)
    pairs = PARTS // 2
    rows = held.shape[0] // PARTS
    for n in range(pairs):
        at = slice(n * rows, (n + 1) * rows)
        send_ref[at] = held[pl.ds(pl.multiple_of((2 * n + 1 - core) * rows, 8), rows)].astype(
            jnp.bfloat16
        )
        keep_ref[at] = held[pl.ds(pl.multiple_of((2 * n + core) * rows, 8), rows)].astype(
            jnp.bfloat16
        )


def backward_kernel(*refs):
    w_ref, turned_ref = refs[:2]
    grads, refs = refs[2 : SEQ + 2], refs[SEQ + 2 :]
    key_parts, value_parts, refs = refs[:SEQ], refs[SEQ : 2 * SEQ], refs[2 * SEQ :]
    q_ref, k_ref, v_ref, send_ref, keep_ref, dpacked, held = refs
    length, width = dpacked.shape[0], turned_ref.shape[0]
    unit = unit_of(grads, length * width)
    factor = 1.0 / math.sqrt(HEAD_DIM) * unit
    slots = value_parts[0].shape[0]
    span = slots * SEQ
    keys = [p[:slots] for p in key_parts] + [k_ref[...]]
    values = [p[...] for p in value_parts] + [v_ref[...]]
    count = length // SEQ
    dkey = jnp.zeros((HEAD_DIM, length), jnp.float32)
    dvalue = jnp.zeros((HEAD_DIM, length), jnp.float32)
    per = 2
    for r in range(SEQ // per):
        rows = slice(r * per * count, (r + 1) * per * count)
        dmixed = jnp.concatenate([g[:count] for g in grads[r * per : (r + 1) * per]], axis=0)
        weights = [w_ref[0, rows, n * slots : (n + 1) * slots] for n in range(SEQ)]
        weights.append(w_ref[0, rows, span:])
        dprobs = [dot(dmixed, v, NT) for v in values]
        inner = sum(
            jnp.sum(p.astype(jnp.float32) * d, axis=-1, keepdims=True)
            for p, d in zip(weights, dprobs)
        )
        dscores = [
            (p.astype(jnp.float32) * (d - inner) * factor).astype(jnp.bfloat16)
            for p, d in zip(weights, dprobs)
        ]
        dquery = sum(dot(d, k) for d, k in zip(dscores, keys))
        dpacked[rows, :HEAD_DIM] = dquery.astype(jnp.bfloat16)
        dkey += dot(q_ref[rows], dscores[SEQ], TN)
        dvalue += dot(dmixed, weights[SEQ], TN)
    dpacked[:, HEAD_DIM : 2 * HEAD_DIM] = dkey.astype(jnp.bfloat16).T
    dpacked[:, 2 * HEAD_DIM :] = (dvalue * unit).astype(jnp.bfloat16).T
    held[...] = dot(turned_ref[...], dpacked[...])
    split_rows(held, send_ref, keep_ref)


def backward(weights, turned, grads, key_parts, value_parts, packed):
    heads, length, total = weights.shape
    width = turned.shape[0]
    slots = value_parts[0].shape[0]
    part = lambda rows: pl.BlockSpec((rows, HEAD_DIM), lambda h: (0, h))
    half = pl.BlockSpec((width // 2, 3 * HEAD_DIM), lambda h: (0, h))
    return pl.pallas_call(
        backward_kernel,
        grid=(heads,),
        in_specs=[pl.BlockSpec((1, length, total), lambda h: (h, 0, 0))]
        + [pl.BlockSpec((width, length), lambda h: (0, 0))]
        + [part(grads[0].shape[0])] * SEQ
        + [part(key_parts[0].shape[0])] * SEQ
        + [part(slots)] * SEQ
        + [pl.BlockSpec((length, HEAD_DIM), lambda h, j=j: (0, 3 * h + j)) for j in range(3)],
        out_specs=[half] * 2,
        out_shape=[far_out((width // 2, packed.shape[1]))] * 2,
        scratch_shapes=[
            pltpu.VMEM((length, 3 * HEAD_DIM), jnp.bfloat16),
            pltpu.VMEM((width, 3 * HEAD_DIM), jnp.float32),
        ],
        compiler_params=within(26),
        name="backward",
    )(
        *near(weights, turned, *grads),
        *far(*key_parts, *value_parts),
        *near(packed, packed, packed),
    )


def out_grad_kernel(*refs):
    grads, gaps, mixed = refs[:SEQ], refs[SEQ : 2 * SEQ], refs[2 * SEQ : 3 * SEQ]
    send_ref, keep_ref, held = refs[3 * SEQ :]
    total = dot(gaps[0][...], mixed[0][...], TN)
    for k in range(1, SEQ):
        total += dot(gaps[k][...], mixed[k][...], TN)
    entries = gaps[0].shape[0] * SEQ * gaps[0].shape[1]
    held[...] = total * unit_of(grads, entries)
    split_rows(held, send_ref, keep_ref)


def out_gradient(grads, gaps, mixed):
    width, features = gaps[0].shape[1], mixed[0].shape[1]
    return pl.pallas_call(
        out_grad_kernel,
        in_specs=[VMEM] * (3 * SEQ),
        out_specs=[VMEM] * 2,
        out_shape=[far_out((width // 2, features))] * 2,
        scratch_shapes=[pltpu.VMEM((width, features), jnp.float32)],
        compiler_params=within(16),
        name="out_gradient",
    )(*near(*grads), *far(*gaps, *mixed))


def chip_sum(send, keep):
    arrived = lax.ppermute(send, "dp", [(i, i ^ 1) for i in range(PARTS)])
    return (keep.astype(jnp.float32) + arrived.astype(jnp.float32)).astype(jnp.bfloat16)


def summed_over_chips(x):
    pieces = x.reshape(PARTS // 2, x.shape[0] * 2 // PARTS, x.shape[1])
    arrived = lax.all_to_all(
        pieces, "dp", split_axis=0, concat_axis=0, tiled=True, axis_index_groups=chip_groups()
    )
    return arrived.astype(jnp.float32).sum(axis=0)


def shards(
    latents,
    fresh_noise,
    cache_key,
    cache_value,
    cache_frame,
    block_index,
    timestep,
    gain_gen,
    w_qkv,
    w_out,
    gain_real,
    w_real,
    gain_fake,
    w_fake,
):
    position = lax.axis_index("seq")
    replica = lax.axis_index("dp")
    latents, fresh_noise = latents[0], fresh_noise[0]
    cache_key, cache_value = cache_key[0], cache_value[0]
    count, width = latents.shape
    slots = cache_key.shape[0]
    features = w_out.shape[0]
    heads_here = features // HEAD_DIM

    slice_at = jnp.reshape((replica // 4) * 2 + replica % 2, (1,)).astype(jnp.int32)
    own = weight_slices(w_out.T, w_real, w_fake, slice_at, width // (PARTS // 2))
    parts = [own] + [shifted(own, -k) for k in range(1, SEQ)]
    slices = placed(parts)
    whole = lax.all_gather(slices, "dp", axis=1, tiled=True, axis_index_groups=plane_groups())

    half = count // 2
    before, after = shifted(latents, 1), shifted(latents, -1)
    tokens = [latents, before, shifted(before[:half], 1), shifted(after[half:], -1), after]
    start = block_index[0] * FRAMES
    open_slots = (cache_frame >= start - WINDOW_FRAMES) & (cache_frame < start)
    flags = open_slots.astype(jnp.bfloat16).reshape(slots // HEAD_DIM, HEAD_DIM)
    flags = jnp.pad(jnp.tile(flags, (1, heads_here)), ((0, 8 - slots // HEAD_DIM), (0, 0)))

    def exchanged(make):
        return [make(position)] + [shifted(make(position + k), k) for k in range(1, SEQ)]

    key_parts = exchanged(lambda j: jnp.concatenate([block_of(cache_key, j, 1), flags], axis=0))
    value_parts = exchanged(lambda j: block_of(cache_value, j, 1))
    turned, packed = project(tokens, gain_gen, w_qkv)
    weights = attention_weights(key_parts, packed)
    mixed = attention_mix(weights, value_parts, packed)

    back = [mixed[0]] + [shifted(mixed[k], -k) for k in range(1, SEQ)]
    angle = math.pi / 2 * timestep.astype(jnp.float32) / 1000.0
    blend = jnp.broadcast_to(jnp.stack([jnp.cos(angle), jnp.sin(angle)]), (2, HEAD_DIM))
    clean, gap, *dmixed = middle(
        blend, back, latents, fresh_noise, gain_real, gain_fake, whole
    )
    grads = [dmixed[0]] + [shifted(dmixed[k], k) for k in range(1, SEQ)]
    gaps = [gap] + [shifted(gap, k) for k in range(1, SEQ)]
    halves = backward(weights, turned, grads, key_parts, value_parts, packed)
    qkv = chip_sum(*halves)
    halves = out_gradient(grads, gaps, mixed)
    outg = chip_sum(*halves)
    first = 2 * 3 * HEAD_DIM
    share_a = summed_over_chips(qkv[:, :first])
    share_b = summed_over_chips(jnp.concatenate([qkv[:, first:], outg], axis=1))
    rest = qkv.shape[1] - first
    qkv_share = jnp.concatenate([share_a, share_b[:, :rest]], axis=1)
    return (clean[None], qkv_share, share_b[:, rest:].T)


def solution(mesh):
    in_specs = (
        P("dp", "seq", None),
        P("dp", "seq", None),
        P("dp", "seq", None),
        P("dp", "seq", None),
        P("dp", "seq"),
        P(),
        P("dp"),
        P(),
        P(None, "seq"),
        P("seq", None),
        P(),
        P(None, "seq"),
        P(),
        P(None, "seq"),
    )
    out_specs = (P("dp", "seq", None), P("dp", "seq"), P("seq", "dp"))

    return jax.shard_map(shards, mesh=mesh, in_specs=in_specs, out_specs=out_specs, check_vma=False)
```

profile of v0, /device:TPU:1, one launch (start us, length us, event | category | flops | bytes accessed | tf_op | source)
XLA Modules:
  0.0 263.2 jit_solution(9591771201368063599)
XLA Ops:
  11.2 3.8 %collective-permute-start.15 = (bf16[3,48,384]{2,1,0:T(8,128)(2,1)}, bf16[3,48,384]{2,1,0:T(8,128)(2,1)S(1)}, u32[]{:S(2)}, u32[]{:S(2)}) collective-permute-start(bf16[3,48,384]{2,1,0:T(8,128)(2,1)} %weight_slices.1.refs_0_), channel_id=1, source_target_pairs={{0,1},{1,2},{2,3},{3,0},{4,5},{5,6},{6,7},{7,4},{8,9},{9,10},{10,1... | collective-permute-start | bytes 331784 | tf_op jit(solution)/shard_map/ppermute | solution.py:20
  15.0 5.1 %collective-permute-start.14 = (bf16[3,48,384]{2,1,0:T(8,128)(2,1)}, bf16[3,48,384]{2,1,0:T(8,128)(2,1)S(1)}, u32[]{:S(2)}, u32[]{:S(2)}) collective-permute-start(bf16[3,48,384]{2,1,0:T(8,128)(2,1)} %weight_slices.1.refs_0_), channel_id=1, source_target_pairs={{0,2},{1,3},{2,0},{3,1},{4,6},{5,7},{6,4},{7,5},{8,10},{9,11},{10,... | collective-permute-start | bytes 331784 | tf_op jit(solution)/shard_map/ppermute | solution.py:20
  22.5 5.1 %collective-permute-done.14.refs_2_ = bf16[3,48,384]{2,1,0:T(8,128)(2,1)S(1)} collective-permute-done((bf16[3,48,384]{2,1,0:T(8,128)(2,1)}, bf16[3,48,384]{2,1,0:T(8,128)(2,1)S(1)}, u32[]{:S(2)}, u32[]{:S(2)}) %collective-permute-start.14) | collective-permute-done | bytes 110624 | tf_op jit(solution)/shard_map/ppermute | solution.py:20
  27.6 3.8 %collective-permute-done.13.refs_1_ = bf16[3,48,384]{2,1,0:T(8,128)(2,1)S(1)} collective-permute-done((bf16[3,48,384]{2,1,0:T(8,128)(2,1)}, bf16[3,48,384]{2,1,0:T(8,128)(2,1)S(1)}, u32[]{:S(2)}, u32[]{:S(2)}) %collective-permute-start.13) | collective-permute-done | bytes 110624 | tf_op jit(solution)/shard_map/ppermute | solution.py:20
  33.9 3.4 %collective-permute-start.5 = (bf16[128,1536]{1,0:T(8,128)(2,1)S(1)}, bf16[128,1536]{1,0:T(8,128)(2,1)S(1)}, u32[]{:S(2)}, u32[]{:S(2)}) collective-permute-start(bf16[128,1536]{1,0:T(8,128)(2,1)S(1)} %bitcast.43), channel_id=1, source_target_pairs={{0,3},{1,0},{2,1},{3,2},{4,7},{5,4},{6,5},{7,6},{8,11},{9,8},{10,9... | collective-permute-start | bytes 1179656 | tf_op jit(solution)/shard_map/ppermute | solution.py:20
  39.0 3.6 %collective-permute-start.2 = (bf16[264,384]{1,0:T(8,128)(2,1)S(1)}, bf16[264,384]{1,0:T(8,128)(2,1)S(1)}, u32[]{:S(2)}, u32[]{:S(2)}) collective-permute-start(bf16[264,384]{1,0:T(8,128)(2,1)S(1)} %get-tuple-element.45), channel_id=1, source_target_pairs={{0,3},{1,0},{2,1},{3,2},{4,7},{5,4},{6,5},{7,6},{8,11},{9,8},{10,9... | collective-permute-start | bytes 608264 | tf_op jit(solution)/shard_map/ppermute | solution.py:20
  42.5 19.0 %collective-permute-done.5.refs_4_ = bf16[128,1536]{1,0:T(8,128)(2,1)S(1)} collective-permute-done((bf16[128,1536]{1,0:T(8,128)(2,1)S(1)}, bf16[128,1536]{1,0:T(8,128)(2,1)S(1)}, u32[]{:S(2)}, u32[]{:S(2)}) %collective-permute-start.5) | collective-permute-done | bytes 393248 | tf_op jit(solution)/shard_map/ppermute | solution.py:20
  82.2 5.4 %project.1 = (bf16[1536,512]{1,0:T(8,128)(2,1)S(1)}, bf16[512,1152]{1,0:T(8,128)(2,1)S(1)}) custom-call(bf16[128,1536]{1,0:T(8,128)(2,1)} %bitcast.41, bf16[128,1536]{1,0:T(8,128)(2,1)} %copy-done.4, bf16[64,1536]{1,0:T(8,128)(2,1)} %copy-done.18, bf16[64,1536]{1,0:T(8,128)(2,1)} %copy-done.17, bf16[128,1536]{1,0:T(8,128)(2,1)} %copy-done.3, ...), custom_call_target="tpu_custom_call" | custom-call | tf_op jit(solution)/shard_map/project/pallas_call | solution.py:134
  88.3 5.1 %attention_weights.1.refs_0_ = bf16[3,512,1536]{2,1,0:T(8,128)(2,1)S(1)} custom-call(bf16[264,384]{1,0:T(8,128)(2,1)} %get-tuple-element.46.refs_0_.refs_6_, bf16[264,384]{1,0:T(8,128)(2,1)} %copy-done.6, bf16[264,384]{1,0:T(8,128)(2,1)} %copy-done.7, bf16[264,384]{1,0:T(8,128)(2,1)} %copy-done.5, ...), custom_call_target="tpu_custom_call" | custom-call | tf_op jit(solution)/shard_map/attention_weights/pallas_call | solution.py:180
  93.5 3.8 %collective-permute-done.8.refs_3_.refs_12_ = bf16[256,384]{1,0:T(8,128)(2,1)S(1)} collective-permute-done((bf16[256,384]{1,0:T(8,128)(2,1)S(1)}, bf16[256,384]{1,0:T(8,128)(2,1)S(1)}, u32[]{:S(2)}, u32[]{:S(2)}) %collective-permute-start.8) | collective-permute-done | bytes 196640 | tf_op jit(solution)/shard_map/ppermute | solution.py:20
  98.0 3.7 %attention_mix.1 = (bf16[128,384]{1,0:T(8,128)(2,1)}, bf16[128,384]{1,0:T(8,128)(2,1)}, bf16[128,384]{1,0:T(8,128)(2,1)}, bf16[128,384]{1,0:T(8,128)(2,1)}) custom-call(bf16[3,512,1536]{2,1,0:T(8,128)(2,1)S(1)} %attention_weights.1.refs_0_, bf16[256,384]{1,0:T(8,128)(2,1)} %get-tuple-element.37.refs_1_.refs_10_, bf16[256,384]{1,0:T(8,128)(2,1)} %copy-done.9, ...), custom_call_target="tpu_custom_call" | custom-call | tf_op jit(solution)/shard_map/attention_mix/pallas_call | solution.py:208
  103.7 6.2 %collective-permute-start.11 = (bf16[128,384]{1,0:T(8,128)(2,1)}, bf16[128,384]{1,0:T(8,128)(2,1)S(1)}, u32[]{:S(2)}, u32[]{:S(2)}) collective-permute-start(bf16[128,384]{1,0:T(8,128)(2,1)} %get-tuple-element.22.refs_10_), channel_id=1, source_target_pairs={{0,2},{1,3},{2,0},{3,1},{4,6},{5,7},{6,4},{7,5},{8,10},{9,11},{10,... | collective-permute-start | bytes 294920 | tf_op jit(solution)/shard_map/ppermute | solution.py:20
  112.6 4.8 %collective-permute-done.12.refs_3_ = bf16[128,384]{1,0:T(8,128)(2,1)S(1)} collective-permute-done((bf16[128,384]{1,0:T(8,128)(2,1)}, bf16[128,384]{1,0:T(8,128)(2,1)S(1)}, u32[]{:S(2)}, u32[]{:S(2)}) %collective-permute-start.12) | collective-permute-done | bytes 98336 | tf_op jit(solution)/shard_map/ppermute | solution.py:20
  118.1 9.3 %middle.1 = (bf16[128,1536]{1,0:T(8,128)(2,1)}, bf16[128,1536]{1,0:T(8,128)(2,1)}, bf16[136,384]{1,0:T(8,128)(2,1)S(1)}, bf16[136,384]{1,0:T(8,128)(2,1)S(1)}, b...) custom-call(bf16[128,384]{1,0:T(8,128)(2,1)} %get-tuple-element.20.refs_0_.refs_8_, ...), custom_call_target="tpu_custom_call" | custom-call | tf_op jit(solution)/shard_map/middle/pallas_call | solution.py:282
  136.2 11.9 %backward.1 = (bf16[768,1152]{1,0:T(8,128)(2,1)}, bf16[768,1152]{1,0:T(8,128)(2,1)}) custom-call(bf16[3,512,1536]{2,1,0:T(8,128)(2,1)S(1)} %bitcast.37, bf16[1536,512]{1,0:T(8,128)(2,1)S(1)} %get-tuple-element.25.refs_1_, bf16[136,384]{1,0:T(8,128)(2,1)S(1)} %get-tuple-element.26.refs_2_.refs_0_, ...), custom_call_target="tpu_custom_call" | custom-call | tf_op jit(solution)/shard_map/backward/pallas_call | solution.py:357
  148.1 7.2 %collective-permute-start.19 = (bf16[768,1152]{1,0:T(8,128)(2,1)}, bf16[768,1152]{1,0:T(8,128)(2,1)S(1)}, u32[]{:S(2)}, u32[]{:S(2)}) collective-permute-start(bf16[768,1152]{1,0:T(8,128)(2,1)} %get-tuple-element.31), channel_id=1, source_target_pairs={{0,4},{4,0},{8,12},{12,8},{16,20},{20,16},{24,28},{28,24},{32,36},... | collective-permute-start | bytes 5308424 | tf_op jit(solution)/shard_map/ppermute | solution.py:406
  160.7 22.6 %collective-permute-done.22.refs_7_ = bf16[128,1536]{1,0:T(8,128)(2,1)S(1)} collective-permute-done((bf16[128,1536]{1,0:T(8,128)(2,1)S(1)}, bf16[128,1536]{1,0:T(8,128)(2,1)S(1)}, u32[]{:S(2)}, u32[]{:S(2)}) %collective-permute-start.22) | collective-permute-done | bytes 393248 | tf_op jit(solution)/shard_map/ppermute | solution.py:20
  183.3 4.5 %collective-permute-done.21.refs_6_ = bf16[128,1536]{1,0:T(8,128)(2,1)S(1)} collective-permute-done((bf16[128,1536]{1,0:T(8,128)(2,1)S(1)}, bf16[128,1536]{1,0:T(8,128)(2,1)S(1)}, u32[]{:S(2)}, u32[]{:S(2)}) %collective-permute-start.21) | collective-permute-done | bytes 393248 | tf_op jit(solution)/shard_map/ppermute | solution.py:20
  187.8 7.7 %collective-permute-done.20.refs_5_ = bf16[128,1536]{1,0:T(8,128)(2,1)S(1)} collective-permute-done((bf16[128,1536]{1,0:T(8,128)(2,1)S(1)}, bf16[128,1536]{1,0:T(8,128)(2,1)S(1)}, u32[]{:S(2)}, u32[]{:S(2)}) %collective-permute-start.20) | collective-permute-done | bytes 393248 | tf_op jit(solution)/shard_map/ppermute | solution.py:20
  196.3 4.6 %out_gradient.1 = (bf16[768,384]{1,0:T(8,128)(2,1)}, bf16[768,384]{1,0:T(8,128)(2,1)}) custom-call(bf16[136,384]{1,0:T(8,128)(2,1)S(1)} %get-tuple-element.26.refs_2_.refs_0_, bf16[136,384]{1,0:T(8,128)(2,1)S(1)} %collective-permute-done.16.refs_3_.refs_1_, bf16[136,384]{1,0:T(8,128)(2,1)S(1)} %collective-permute-done.17.refs_4_.refs_2_, ...), custom_call_target="tpu_custom_call" | custom-call | tf_op jit(solution)/shard_map/out_gradient/pallas_call | solution.py:394
  206.5 9.3 %all-to-all-start.1 = ((bf16[32,24,768]{2,1,0:T(8,128)(2,1)}), bf16[32,24,768]{2,1,0:T(8,128)(2,1)S(1)}, u32[]{:S(2)}, u32[]{:S(2)}) async-start(bf16[32,24,768]{2,1,0:T(8,128)(2,1)} %bitcast.40), calls=%async_computation.1 | async-start | bytes 2359296 | tf_op jit(solution)/shard_map/all_to_all | solution.py:412
  216.9 17.3 %all-to-all-done.1 = bf16[32,24,768]{2,1,0:T(8,128)(2,1)S(1)} async-done(((bf16[32,24,768]{2,1,0:T(8,128)(2,1)}), bf16[32,24,768]{2,1,0:T(8,128)(2,1)S(1)}, u32[]{:S(2)}, u32[]{:S(2)}) %all-to-all-start.1) | async-done | bytes 1179680 | tf_op jit(solution)/shard_map/all_to_all | solution.py:412
  234.2 3.9 %all-to-all-start = ((bf16[32,24,768]{2,1,0:T(8,128)(2,1)}), bf16[32,24,768]{2,1,0:T(8,128)(2,1)S(1)}, u32[]{:S(2)}, u32[]{:S(2)}) async-start(bf16[32,24,768]{2,1,0:T(8,128)(2,1)} %bitcast.39), calls=%async_computation | async-start | bytes 2359296 | tf_op jit(solution)/shard_map/all_to_all | solution.py:412
  238.9 16.6 %all-to-all-done = bf16[32,24,768]{2,1,0:T(8,128)(2,1)S(1)} async-done(((bf16[32,24,768]{2,1,0:T(8,128)(2,1)}), bf16[32,24,768]{2,1,0:T(8,128)(2,1)S(1)}, u32[]{:S(2)}, u32[]{:S(2)}) %all-to-all-start) | async-done | bytes 1179680 | tf_op jit(solution)/shard_map/all_to_all | solution.py:412
  (125 shorter events, 59.6 us)
Async XLA Ops:
  7.2 110.2 %all-gather.2.cloned.1.call-start = ((), (), s32[]{:S(2)}) async-start(), calls=%async_computation.2 | async-start | bytes 14598144 | tf_op jit(solution)/shard_map/all_gather | solution.py:447
  11.2 11.3 %collective-permute-start.15 = (bf16[3,48,384]{2,1,0:T(8,128)(2,1)}, bf16[3,48,384]{2,1,0:T(8,128)(2,1)S(1)}, u32[]{:S(2)}, u32[]{:S(2)}) collective-permute-start(bf16[3,48,384]{2,1,0:T(8,128)(2,1)} %weight_slices.1.refs_0_), channel_id=1, source_target_pairs={{0,1},{1,2},{2,3},{3,0},{4,5},{5,6},{6,7},{7,4},{8,9},{9,10},{10,1... | collective-permute-start | bytes 331784 | tf_op jit(solution)/shard_map/ppermute | solution.py:20
  15.0 12.6 %collective-permute-start.14 = (bf16[3,48,384]{2,1,0:T(8,128)(2,1)}, bf16[3,48,384]{2,1,0:T(8,128)(2,1)S(1)}, u32[]{:S(2)}, u32[]{:S(2)}) collective-permute-start(bf16[3,48,384]{2,1,0:T(8,128)(2,1)} %weight_slices.1.refs_0_), channel_id=1, source_target_pairs={{0,2},{1,3},{2,0},{3,1},{4,6},{5,7},{6,4},{7,5},{8,10},{9,11},{10,... | collective-permute-start | bytes 331784 | tf_op jit(solution)/shard_map/ppermute | solution.py:20
  20.1 11.3 %collective-permute-start.13 = (bf16[3,48,384]{2,1,0:T(8,128)(2,1)}, bf16[3,48,384]{2,1,0:T(8,128)(2,1)S(1)}, u32[]{:S(2)}, u32[]{:S(2)}) collective-permute-start(bf16[3,48,384]{2,1,0:T(8,128)(2,1)} %weight_slices.1.refs_0_), channel_id=1, source_target_pairs={{0,3},{1,0},{2,1},{3,2},{4,7},{5,4},{6,5},{7,6},{8,11},{9,8},{10,9... | collective-permute-start | bytes 331784 | tf_op jit(solution)/shard_map/ppermute | solution.py:20
  33.9 27.6 %collective-permute-start.5 = (bf16[128,1536]{1,0:T(8,128)(2,1)S(1)}, bf16[128,1536]{1,0:T(8,128)(2,1)S(1)}, u32[]{:S(2)}, u32[]{:S(2)}) collective-permute-start(bf16[128,1536]{1,0:T(8,128)(2,1)S(1)} %bitcast.43), channel_id=1, source_target_pairs={{0,3},{1,0},{2,1},{3,2},{4,7},{5,4},{6,5},{7,6},{8,11},{9,8},{10,9... | collective-permute-start | bytes 1179656 | tf_op jit(solution)/shard_map/ppermute | solution.py:20
  37.3 27.6 %collective-permute-start.3 = (bf16[128,1536]{1,0:T(8,128)(2,1)S(1)}, bf16[128,1536]{1,0:T(8,128)(2,1)S(1)}, u32[]{:S(2)}, u32[]{:S(2)}) collective-permute-start(bf16[128,1536]{1,0:T(8,128)(2,1)S(1)} %bitcast.44), channel_id=1, source_target_pairs={{0,1},{1,2},{2,3},{3,0},{4,5},{5,6},{6,7},{7,4},{8,9},{9,10},{10,1... | collective-permute-start | bytes 1179656 | tf_op jit(solution)/shard_map/ppermute | solution.py:20
  39.0 32.4 %collective-permute-start.2 = (bf16[264,384]{1,0:T(8,128)(2,1)S(1)}, bf16[264,384]{1,0:T(8,128)(2,1)S(1)}, u32[]{:S(2)}, u32[]{:S(2)}) collective-permute-start(bf16[264,384]{1,0:T(8,128)(2,1)S(1)} %get-tuple-element.45), channel_id=1, source_target_pairs={{0,3},{1,0},{2,1},{3,2},{4,7},{5,4},{6,5},{7,6},{8,11},{9,8},{10,9... | collective-permute-start | bytes 608264 | tf_op jit(solution)/shard_map/ppermute | solution.py:20
  61.6 12.5 %collective-permute-start.6 = (bf16[64,1536]{1,0:T(8,128)(2,1)S(1)}, bf16[64,1536]{1,0:T(8,128)(2,1)S(1)}, u32[]{:S(2)}, u32[]{:S(2)}) collective-permute-start(bf16[64,1536]{1,0:T(8,128)(2,1)S(1)} %slice.25), channel_id=1, source_target_pairs={{0,3},{1,0},{2,1},{3,2},{4,7},{5,4},{6,5},{7,6},{8,11},{9,8},{10,9... | collective-permute-start | bytes 589832 | tf_op jit(solution)/shard_map/ppermute | solution.py:20
  64.9 11.3 %collective-permute-start.4 = (bf16[64,1536]{1,0:T(8,128)(2,1)S(1)}, bf16[64,1536]{1,0:T(8,128)(2,1)S(1)}, u32[]{:S(2)}, u32[]{:S(2)}) collective-permute-start(bf16[64,1536]{1,0:T(8,128)(2,1)S(1)} %slice.24), channel_id=1, source_target_pairs={{0,1},{1,2},{2,3},{3,0},{4,5},{5,6},{6,7},{7,4},{8,9},{9,10},{10,1... | collective-permute-start | bytes 589832 | tf_op jit(solution)/shard_map/ppermute | solution.py:20
  65.0 22.6 %collective-permute-start = (bf16[264,384]{1,0:T(8,128)(2,1)S(1)}, bf16[264,384]{1,0:T(8,128)(2,1)S(1)}, u32[]{:S(2)}, u32[]{:S(2)}) collective-permute-start(bf16[264,384]{1,0:T(8,128)(2,1)S(1)} %get-tuple-element.47), channel_id=1, source_target_pairs={{0,1},{1,2},{2,3},{3,0},{4,5},{5,6},{6,7},{7,4},{8,9},{9,10},{10,1... | collective-permute-start | bytes 608264 | tf_op jit(solution)/shard_map/ppermute | solution.py:20
  67.8 19.8 %collective-permute-start.1 = (bf16[264,384]{1,0:T(8,128)(2,1)S(1)}, bf16[264,384]{1,0:T(8,128)(2,1)S(1)}, u32[]{:S(2)}, u32[]{:S(2)}) collective-permute-start(bf16[264,384]{1,0:T(8,128)(2,1)S(1)} %get-tuple-element.48), channel_id=1, source_target_pairs={{0,2},{1,3},{2,0},{3,1},{4,6},{5,7},{6,4},{7,5},{8,10},{9,11},{10,... | collective-permute-start | bytes 608264 | tf_op jit(solution)/shard_map/ppermute | solution.py:20
  71.4 22.0 %collective-permute-start.9 = (bf16[256,384]{1,0:T(8,128)(2,1)S(1)}, bf16[256,384]{1,0:T(8,128)(2,1)S(1)}, u32[]{:S(2)}, u32[]{:S(2)}) collective-permute-start(bf16[256,384]{1,0:T(8,128)(2,1)S(1)} %get-tuple-element.35), channel_id=1, source_target_pairs={{0,3},{1,0},{2,1},{3,2},{4,7},{5,4},{6,5},{7,6},{8,11},{9,8},{10,9... | collective-permute-start | bytes 589832 | tf_op jit(solution)/shard_map/ppermute | solution.py:20
  74.1 19.4 %collective-permute-start.7 = (bf16[256,384]{1,0:T(8,128)(2,1)S(1)}, bf16[256,384]{1,0:T(8,128)(2,1)S(1)}, u32[]{:S(2)}, u32[]{:S(2)}) collective-permute-start(bf16[256,384]{1,0:T(8,128)(2,1)S(1)} %get-tuple-element.36), channel_id=1, source_target_pairs={{0,1},{1,2},{2,3},{3,0},{4,5},{5,6},{6,7},{7,4},{8,9},{9,10},{10,1... | collective-permute-start | bytes 589832 | tf_op jit(solution)/shard_map/ppermute | solution.py:20
  76.3 21.0 %collective-permute-start.8 = (bf16[256,384]{1,0:T(8,128)(2,1)S(1)}, bf16[256,384]{1,0:T(8,128)(2,1)S(1)}, u32[]{:S(2)}, u32[]{:S(2)}) collective-permute-start(bf16[256,384]{1,0:T(8,128)(2,1)S(1)} %get-tuple-element.38), channel_id=1, source_target_pairs={{0,2},{1,3},{2,0},{3,1},{4,6},{5,7},{6,4},{7,5},{8,10},{9,11},{10,... | collective-permute-start | bytes 589832 | tf_op jit(solution)/shard_map/ppermute | solution.py:20
  101.6 8.5 %collective-permute-start.10 = (bf16[128,384]{1,0:T(8,128)(2,1)}, bf16[128,384]{1,0:T(8,128)(2,1)S(1)}, u32[]{:S(2)}, u32[]{:S(2)}) collective-permute-start(bf16[128,384]{1,0:T(8,128)(2,1)} %get-tuple-element.21.refs_9_), channel_id=1, source_target_pairs={{0,3},{1,0},{2,1},{3,2},{4,7},{5,4},{6,5},{7,6},{8,11},{9,8},{10,9... | collective-permute-start | bytes 294920 | tf_op jit(solution)/shard_map/ppermute | solution.py:20
  103.7 8.8 %collective-permute-start.11 = (bf16[128,384]{1,0:T(8,128)(2,1)}, bf16[128,384]{1,0:T(8,128)(2,1)S(1)}, u32[]{:S(2)}, u32[]{:S(2)}) collective-permute-start(bf16[128,384]{1,0:T(8,128)(2,1)} %get-tuple-element.22.refs_10_), channel_id=1, source_target_pairs={{0,2},{1,3},{2,0},{3,1},{4,6},{5,7},{6,4},{7,5},{8,10},{9,11},{10,... | collective-permute-start | bytes 294920 | tf_op jit(solution)/shard_map/ppermute | solution.py:20
  109.9 7.5 %collective-permute-start.12 = (bf16[128,384]{1,0:T(8,128)(2,1)}, bf16[128,384]{1,0:T(8,128)(2,1)S(1)}, u32[]{:S(2)}, u32[]{:S(2)}) collective-permute-start(bf16[128,384]{1,0:T(8,128)(2,1)} %get-tuple-element.23.refs_11_), channel_id=1, source_target_pairs={{0,1},{1,2},{2,3},{3,0},{4,5},{5,6},{6,7},{7,4},{8,9},{9,10},{10,1... | collective-permute-start | bytes 294920 | tf_op jit(solution)/shard_map/ppermute | solution.py:20
  127.5 8.7 %collective-permute-start.17 = (bf16[136,384]{1,0:T(8,128)(2,1)S(1)}, bf16[136,384]{1,0:T(8,128)(2,1)S(1)}, u32[]{:S(2)}, u32[]{:S(2)}) collective-permute-start(bf16[136,384]{1,0:T(8,128)(2,1)S(1)} %get-tuple-element.28), channel_id=1, source_target_pairs={{0,2},{1,3},{2,0},{3,1},{4,6},{5,7},{6,4},{7,5},{8,10},{9,11},{10,... | collective-permute-start | bytes 313352 | tf_op jit(solution)/shard_map/ppermute | solution.py:20
  148.1 56.6 %collective-permute-start.19 = (bf16[768,1152]{1,0:T(8,128)(2,1)}, bf16[768,1152]{1,0:T(8,128)(2,1)S(1)}, u32[]{:S(2)}, u32[]{:S(2)}) collective-permute-start(bf16[768,1152]{1,0:T(8,128)(2,1)} %get-tuple-element.31), channel_id=1, source_target_pairs={{0,4},{4,0},{8,12},{12,8},{16,20},{20,16},{24,28},{28,24},{32,36},... | collective-permute-start | bytes 5308424 | tf_op jit(solution)/shard_map/ppermute | solution.py:406
  155.3 28.0 %collective-permute-start.22 = (bf16[128,1536]{1,0:T(8,128)(2,1)S(1)}, bf16[128,1536]{1,0:T(8,128)(2,1)S(1)}, u32[]{:S(2)}, u32[]{:S(2)}) collective-permute-start(bf16[128,1536]{1,0:T(8,128)(2,1)S(1)} %copy-done.13), channel_id=1, source_target_pairs={{0,3},{1,0},{2,1},{3,2},{4,7},{5,4},{6,5},{7,6},{8,11},{9,8},{10,9... | collective-permute-start | bytes 1179656 | tf_op jit(solution)/shard_map/ppermute | solution.py:20
  157.4 30.5 %collective-permute-start.21 = (bf16[128,1536]{1,0:T(8,128)(2,1)S(1)}, bf16[128,1536]{1,0:T(8,128)(2,1)S(1)}, u32[]{:S(2)}, u32[]{:S(2)}) collective-permute-start(bf16[128,1536]{1,0:T(8,128)(2,1)S(1)} %copy-done.13), channel_id=1, source_target_pairs={{0,2},{1,3},{2,0},{3,1},{4,6},{5,7},{6,4},{7,5},{8,10},{9,11},{10,... | collective-permute-start | bytes 1179656 | tf_op jit(solution)/shard_map/ppermute | solution.py:20
  160.7 34.8 %collective-permute-start.20 = (bf16[128,1536]{1,0:T(8,128)(2,1)S(1)}, bf16[128,1536]{1,0:T(8,128)(2,1)S(1)}, u32[]{:S(2)}, u32[]{:S(2)}) collective-permute-start(bf16[128,1536]{1,0:T(8,128)(2,1)S(1)} %copy-done.13), channel_id=1, source_target_pairs={{0,1},{1,2},{2,3},{3,0},{4,5},{5,6},{6,7},{7,4},{8,9},{9,10},{10,1... | collective-permute-start | bytes 1179656 | tf_op jit(solution)/shard_map/ppermute | solution.py:20
  206.5 27.7 %all-to-all-start.1 = ((bf16[32,24,768]{2,1,0:T(8,128)(2,1)}), bf16[32,24,768]{2,1,0:T(8,128)(2,1)S(1)}, u32[]{:S(2)}, u32[]{:S(2)}) async-start(bf16[32,24,768]{2,1,0:T(8,128)(2,1)} %bitcast.40), calls=%async_computation.1 | async-start | bytes 2359296 | tf_op jit(solution)/shard_map/all_to_all | solution.py:412
  234.2 21.3 %all-to-all-start = ((bf16[32,24,768]{2,1,0:T(8,128)(2,1)}), bf16[32,24,768]{2,1,0:T(8,128)(2,1)S(1)}, u32[]{:S(2)}, u32[]{:S(2)}) async-start(bf16[32,24,768]{2,1,0:T(8,128)(2,1)} %bitcast.39), calls=%async_computation | async-start | bytes 2359296 | tf_op jit(solution)/shard_map/all_to_all | solution.py:412
  (34 other events, 494.9 us)
Sparse Core Ops, SparseCore 0:
  34.0 71.8 all-gather.1
where the time goes:
time: 264 us; the launch traced here: 263 us
  waiting for transfers between devices  115 us (44%)
  starting transfers between devices  74 us (28%)
  Pallas kernels  43.4 us (16%)
  between operations  15.9 us (6%)
  local copies, waits for them, and re-layouts  10.4 us (4%)
  other arithmetic  4.72 us (2%)
    ppermute x22, waiting for transfers between devices, shifted(): return lax.ppermute(x, 'seq', [(i, (i + by) % SEQ) for i in range(SEQ)])  79 us
    ppermute x22, starting transfers between devices, shifted(): return lax.ppermute(x, 'seq', [(i, (i + by) % SEQ) for i in range(SEQ)])  52.8 us
    all_to_all x2, waiting for transfers between devices, summed_over_chips(): lax.all_to_all(pieces, 'dp', split_axis=0, concat_axis=0, tiled=True, axi...  33.9 us
    all_to_all x2, starting transfers between devices, summed_over_chips(): lax.all_to_all(pieces, 'dp', split_axis=0, concat_axis=0, tiled=True, axi...  13.2 us
    pallas_call x1, Pallas kernels, backward(): pl.pallas_call(backward_kernel, grid=(heads,), in_specs=[pl.BlockSpec((1,...  11.9 us
    pallas_call x1, Pallas kernels, middle(): pl.pallas_call(middle_kernel, in_specs=[VMEM] * (SEQ + 5) + [ANY], out_sp...  9.31 us
    ppermute x2, starting transfers between devices, chip_sum(): arrived = lax.ppermute(send, 'dp', [(i, i ^ 1) for i in range(PARTS)])  7.96 us
    pallas_call x1, Pallas kernels, project(): pl.pallas_call(project_kernel, in_specs=[VMEM] * (len(parts) + 2), out_sp...  5.41 us
  transfers between devices with their start and end apart: 27, of which 16 were waited for; matrix products, arithmetic and copies ran while one was open for 3% of the time, Pallas kernels for 7%

commit v1 on v0

--- a/solution.py
+++ b/solution.py
@@ -81,16 +81,18 @@
 
 
 def weight_slices(a, b, c, at, rows):
-    spec = pl.BlockSpec((rows, a.shape[1]), lambda i, at: (at[0], 0))
+    width = b.shape[1]
+    first = pl.BlockSpec((rows, width), lambda i, at: (at[0] // SEQ, at[0] % SEQ))
+    spec = pl.BlockSpec((rows, width), lambda i, at: (at[0], 0))
     return pl.pallas_call(
         slices_kernel,
         grid_spec=pltpu.PrefetchScalarGridSpec(
             num_scalar_prefetch=1,
             grid=(1,),
-            in_specs=[spec] * 3,
-            out_specs=pl.BlockSpec((3, rows, a.shape[1]), lambda i, at: (0, 0, 0)),
+            in_specs=[first, spec, spec],
+            out_specs=pl.BlockSpec((3, rows, width), lambda i, at: (0, 0, 0)),
         ),
-        out_shape=far_out((3, rows, a.shape[1])),
+        out_shape=far_out((3, rows, width)),
         name="weight_slices",
     )(at, *far(a, b, c))
 
@@ -154,8 +156,10 @@
         for p in parts
     ]
     step = 128
-    for r in range(q_ref.shape[0] // step):
-        rows = slice(r * step, (r + 1) * step)
+
+    @pl.loop(0, q_ref.shape[0] // step)
+    def _(r):
+        rows = pl.ds(pl.multiple_of(r * step, step), step)
         query = q_ref[rows]
         scores = [dot(query, k, NT) * factor for k in keys]
         for n in range(SEQ):
@@ -238,20 +242,31 @@
     parts, refs = refs[:SEQ], refs[SEQ:]
     blend_ref, latents_ref, fresh_ref, real_gain_ref, fake_gain_ref, w_ref = refs[:6]
     clean_ref, gap_ref = refs[6:8]
-    outs, (held, sems) = refs[8 : 8 + SEQ], refs[8 + SEQ :]
-    copies = [pltpu.make_async_copy(w_ref.at[n], held.at[n], sems.at[n]) for n in range(3)]
-    for c in copies:
-        c.start()
+    outs, (out_w, held, sems) = refs[8 : 8 + SEQ], refs[8 + SEQ :]
     width = parts[0].shape[1]
 
+    @pl.loop(0, SEQ)
+    def _(j):
+        for c in range(SEQ):
+            pltpu.make_async_copy(
+                w_ref.at[0, :, c, :, pl.ds(pl.multiple_of(j * width, 128), width)],
+                out_w.at[j, :, :, c * width : (c + 1) * width],
+                sems.at[0],
+            ).start()
+
+    copies = [pltpu.make_async_copy(out_w, out_w, sems.at[0])]
+    for n in (1, 2):
+        copies.append(pltpu.make_async_copy(w_ref.at[n], held.at[n - 1], sems.at[n]))
+        copies[n].start()
+
     def block(k):
-        lead = pl.multiple_of(place_in_seq(k) * width, 128)
-        return held[0, :, pl.ds(lead, width)]
+        rows = out_w[place_in_seq(k)]
+        return rows.reshape(width, rows.shape[2])
 
     copies[0].wait()
-    update = dot(parts[0][...], block(0), NT)
+    update = dot(parts[0][...], block(0))
     for k in range(1, SEQ):
-        update += dot(parts[k][...], block(k), NT)
+        update += dot(parts[k][...], block(k))
     clean = (latents_ref[...].astype(jnp.float32) + update).astype(jnp.bfloat16)
     clean_ref[...] = clean
     clean_f = clean.astype(jnp.float32)
@@ -261,19 +276,20 @@
         .astype(jnp.float32)
     )
     scaled = noisy * lax.rsqrt(jnp.mean(noisy * noisy, axis=-1, keepdims=True) + 1e-06)
+    gain_shape = (clean.shape[1], clean.shape[1])
     real_in = (scaled * real_gain_ref[...]).astype(jnp.bfloat16)
     fake_in = (scaled * fake_gain_ref[...]).astype(jnp.bfloat16)
     copies[1].wait()
-    pred_real = noisy + dot(real_in, held[1])
+    pred_real = noisy + dot(real_in, held[0].reshape(gain_shape))
     total = jnp.sum(jnp.abs(clean_f - pred_real), axis=(0, 1), keepdims=True)
     copies[2].wait()
-    pred_fake = noisy + dot(fake_in, held[2])
+    pred_fake = noisy + dot(fake_in, held[1].reshape(gain_shape))
     gap = (pred_fake - pred_real).astype(jnp.bfloat16)
     gap_ref[...] = gap
     count = gap.shape[0]
     terms = in_terms(total, (8, width))
     for k in range(SEQ):
-        outs[k][:count] = dot(gap, block(k)).astype(jnp.bfloat16)
+        outs[k][:count] = dot(gap, block(k), NT).astype(jnp.bfloat16)
         outs[k][count:] = terms
 
 
@@ -285,7 +301,11 @@
         out_specs=[VMEM] * (2 + SEQ),
         out_shape=[far_out((count, width))] * 2
         + [near_out((count + 8, parts[0].shape[1]))] * SEQ,
-        scratch_shapes=[pltpu.VMEM(whole.shape, jnp.bfloat16), pltpu.SemaphoreType.DMA((3,))],
+        scratch_shapes=[
+            pltpu.VMEM((SEQ, whole.shape[1], *whole.shape[3:]), jnp.bfloat16),
+            pltpu.VMEM((2, *whole.shape[1:]), jnp.bfloat16),
+            pltpu.SemaphoreType.DMA((3,)),
+        ],
         compiler_params=within(30),
         name="middle",
     )(
@@ -298,14 +318,13 @@
     core = lax.rem(lax.axis_index("dp"), 2)
     pairs = PARTS // 2
     rows = held.shape[0] // PARTS
-    for n in range(pairs):
-        at = slice(n * rows, (n + 1) * rows)
-        send_ref[at] = held[pl.ds(pl.multiple_of((2 * n + 1 - core) * rows, 8), rows)].astype(
-            jnp.bfloat16
-        )
-        keep_ref[at] = held[pl.ds(pl.multiple_of((2 * n + core) * rows, 8), rows)].astype(
-            jnp.bfloat16
-        )
+
+    @pl.loop(0, pairs)
+    def _(n):
+        at = pl.ds(pl.multiple_of(n * rows, 8), rows)
+        other, own = (2 * n + 1 - core) * rows, (2 * n + core) * rows
+        send_ref[at] = held[pl.ds(pl.multiple_of(other, 8), rows)].astype(jnp.bfloat16)
+        keep_ref[at] = held[pl.ds(pl.multiple_of(own, 8), rows)].astype(jnp.bfloat16)
 
 
 def backward_kernel(*refs):
@@ -348,23 +367,23 @@
     split_rows(held, send_ref, keep_ref)
 
 
-def backward(weights, turned, grads, key_parts, value_parts, packed):
-    heads, length, total = weights.shape
+def backward(first, heads, weights, turned, grads, key_parts, value_parts, packed):
+    length, total = weights.shape[1:]
     width = turned.shape[0]
     slots = value_parts[0].shape[0]
-    part = lambda rows: pl.BlockSpec((rows, HEAD_DIM), lambda h: (0, h))
+    part = lambda rows: pl.BlockSpec((rows, HEAD_DIM), lambda h: (0, first + h))
     half = pl.BlockSpec((width // 2, 3 * HEAD_DIM), lambda h: (0, h))
     return pl.pallas_call(
         backward_kernel,
         grid=(heads,),
-        in_specs=[pl.BlockSpec((1, length, total), lambda h: (h, 0, 0))]
+        in_specs=[pl.BlockSpec((1, length, total), lambda h: (first + h, 0, 0))]
         + [pl.BlockSpec((width, length), lambda h: (0, 0))]
         + [part(grads[0].shape[0])] * SEQ
         + [part(key_parts[0].shape[0])] * SEQ
         + [part(slots)] * SEQ
-        + [pl.BlockSpec((length, HEAD_DIM), lambda h, j=j: (0, 3 * h + j)) for j in range(3)],
+        + [pl.BlockSpec((length, HEAD_DIM), lambda h, j=j: (0, 3 * (first + h) + j)) for j in range(3)],
         out_specs=[half] * 2,
-        out_shape=[far_out((width // 2, packed.shape[1]))] * 2,
+        out_shape=[far_out((width // 2, heads * 3 * HEAD_DIM))] * 2,
         scratch_shapes=[
             pltpu.VMEM((length, 3 * HEAD_DIM), jnp.bfloat16),
             pltpu.VMEM((width, 3 * HEAD_DIM), jnp.float32),
@@ -441,10 +460,11 @@
     heads_here = features // HEAD_DIM
 
     slice_at = jnp.reshape((replica // 4) * 2 + replica % 2, (1,)).astype(jnp.int32)
-    own = weight_slices(w_out.T, w_real, w_fake, slice_at, width // (PARTS // 2))
+    own = weight_slices(w_out, w_real, w_fake, slice_at, width // (PARTS // 2))
     parts = [own] + [shifted(own, -k) for k in range(1, SEQ)]
     slices = placed(parts)
     whole = lax.all_gather(slices, "dp", axis=1, tiled=True, axis_index_groups=plane_groups())
+    whole = whole.reshape(3, PARTS // 2 // SEQ, SEQ, slices.shape[1], width)
 
     half = count // 2
     before, after = shifted(latents, 1), shifted(latents, -1)
@@ -471,14 +491,17 @@
     )
     grads = [dmixed[0]] + [shifted(dmixed[k], k) for k in range(1, SEQ)]
     gaps = [gap] + [shifted(gap, k) for k in range(1, SEQ)]
-    halves = backward(weights, turned, grads, key_parts, value_parts, packed)
-    qkv = chip_sum(*halves)
+    sums = []
+    for heads in (range(0, heads_here - 1), range(heads_here - 1, heads_here)):
+        halves = backward(
+            heads[0], len(heads), weights, turned, grads, key_parts, value_parts, packed
+        )
+        sums.append(chip_sum(*halves))
     halves = out_gradient(grads, gaps, mixed)
     outg = chip_sum(*halves)
-    first = 2 * 3 * HEAD_DIM
-    share_a = summed_over_chips(qkv[:, :first])
-    share_b = summed_over_chips(jnp.concatenate([qkv[:, first:], outg], axis=1))
-    rest = qkv.shape[1] - first
+    share_a = summed_over_chips(sums[0])
+    share_b = summed_over_chips(jnp.concatenate([sums[1], outg], axis=1))
+    rest = sums[1].shape[1]
     qkv_share = jnp.concatenate([share_a, share_b[:, :rest]], axis=1)
     return (clean[None], qkv_share, share_b[:, rest:].T)
 

time: 264 us -> 250 us (0.947)
  waiting for transfers between devices: 115 us -> 91.3 us
  Pallas kernels: 43.4 us -> 46.9 us
  starting transfers between devices: 74 us -> 77.4 us
    all_to_all x2, waiting for transfers between devices: 33.9 us -> 18.9 us  [summed_over_chips(): lax.all_to_all(pieces, 'dp', split_axis=0, concat_axis=0, tiled=True, axi...]
    ppermute x22, waiting for transfers between devices: 79 us -> 67.7 us  [shifted(): return lax.ppermute(x, 'seq', [(i, (i + by) % SEQ) for i in range(SEQ)])]
    all_to_all x2, starting transfers between devices: 13.2 us -> 20.7 us  [summed_over_chips(): lax.all_to_all(pieces, 'dp', split_axis=0, concat_axis=0, tiled=True, axi...]
    ppermute x2 -> x3, starting transfers between devices: 7.96 us -> 1.24 us  [chip_sum(): arrived = lax.ppermute(send, 'dp', [(i, i ^ 1) for i in range(PARTS)])]
    ppermute x2 -> x3, waiting for transfers between devices: 1.84 us -> 4.72 us  [chip_sum(): arrived = lax.ppermute(send, 'dp', [(i, i ^ 1) for i in range(PARTS)])]
    pallas_call x1 -> x2, Pallas kernels: 11.9 us -> 12.9 us  [backward(): pl.pallas_call(backward_kernel, grid=(heads,), in_specs=[pl.BlockSpec((1,...]
    unnamed x65 -> x66, local copies, waits for them, and re-layouts: 5.3 us -> 6.3 us
  transfers between devices with their start and end apart: 27 -> 28, of which waited for: 16 -> 12; matrix products, arithmetic and copies ran while one was open for 3% -> 3% of each run, Pallas kernels for 7% -> 14%
where the time goes in v1:
time: 250 us; the launch traced here: 249 us
  waiting for transfers between devices  91.3 us (37%)
  starting transfers between devices  77.4 us (31%)
  Pallas kernels  46.9 us (19%)
  between operations  15.9 us (6%)
  local copies, waits for them, and re-layouts  10.2 us (4%)
  other arithmetic  7.22 us (3%)
    ppermute x22, waiting for transfers between devices, shifted(): return lax.ppermute(x, 'seq', [(i, (i + by) % SEQ) for i in range(SEQ)])  67.7 us
    ppermute x22, starting transfers between devices, shifted(): return lax.ppermute(x, 'seq', [(i, (i + by) % SEQ) for i in range(SEQ)])  55.4 us
    all_to_all x2, starting transfers between devices, summed_over_chips(): lax.all_to_all(pieces, 'dp', split_axis=0, concat_axis=0, tiled=True, axi...  20.7 us
    all_to_all x2, waiting for transfers between devices, summed_over_chips(): lax.all_to_all(pieces, 'dp', split_axis=0, concat_axis=0, tiled=True, axi...  18.9 us
    pallas_call x2, Pallas kernels, backward(): pl.pallas_call(backward_kernel, grid=(heads,), in_specs=[pl.BlockSpec((1,...  12.9 us
    pallas_call x1, Pallas kernels, middle(): pl.pallas_call(middle_kernel, in_specs=[VMEM] * (SEQ + 5) + [ANY], out_sp...  9.72 us
    pallas_call x1, Pallas kernels, attention_weights(): pl.pallas_call(weights_kernel, grid=(heads,), in_specs=[part] * SEQ + [pl...  7.62 us
    unnamed x66, local copies, waits for them, and re-layouts  6.3 us
  transfers between devices with their start and end apart: 28, of which 12 were waited for; matrix products, arithmetic and copies ran while one was open for 3% of the time, Pallas kernels for 14%

profile of v1, /device:TPU:1, one launch (start us, length us, event | category | flops | bytes accessed | tf_op | source)
XLA Modules:
  0.0 248.9 jit_solution(13884058546958527505)
XLA Ops:
  8.7 3.8 %collective-permute-start.15 = (bf16[3,48,384]{2,1,0:T(8,128)(2,1)}, bf16[3,48,384]{2,1,0:T(8,128)(2,1)S(1)}, u32[]{:S(2)}, u32[]{:S(2)}) collective-permute-start(bf16[3,48,384]{2,1,0:T(8,128)(2,1)} %weight_slices.1.refs_0_), channel_id=1, source_target_pairs={{0,1},{1,2},{2,3},{3,0},{4,5},{5,6},{6,7},{7,4},{8,9},{9,10},{10,1... | collective-permute-start | bytes 331784 | tf_op jit(solution)/shard_map/ppermute | solution.py:20
  12.5 5.1 %collective-permute-start.14 = (bf16[3,48,384]{2,1,0:T(8,128)(2,1)}, bf16[3,48,384]{2,1,0:T(8,128)(2,1)S(1)}, u32[]{:S(2)}, u32[]{:S(2)}) collective-permute-start(bf16[3,48,384]{2,1,0:T(8,128)(2,1)} %weight_slices.1.refs_0_), channel_id=1, source_target_pairs={{0,2},{1,3},{2,0},{3,1},{4,6},{5,7},{6,4},{7,5},{8,10},{9,11},{10,... | collective-permute-start | bytes 331784 | tf_op jit(solution)/shard_map/ppermute | solution.py:20
  20.0 5.1 %collective-permute-done.14.refs_2_ = bf16[3,48,384]{2,1,0:T(8,128)(2,1)S(1)} collective-permute-done((bf16[3,48,384]{2,1,0:T(8,128)(2,1)}, bf16[3,48,384]{2,1,0:T(8,128)(2,1)S(1)}, u32[]{:S(2)}, u32[]{:S(2)}) %collective-permute-start.14) | collective-permute-done | bytes 110624 | tf_op jit(solution)/shard_map/ppermute | solution.py:20
  25.1 3.9 %collective-permute-done.13.refs_1_ = bf16[3,48,384]{2,1,0:T(8,128)(2,1)S(1)} collective-permute-done((bf16[3,48,384]{2,1,0:T(8,128)(2,1)}, bf16[3,48,384]{2,1,0:T(8,128)(2,1)S(1)}, u32[]{:S(2)}, u32[]{:S(2)}) %collective-permute-start.13) | collective-permute-done | bytes 110624 | tf_op jit(solution)/shard_map/ppermute | solution.py:20
  31.5 3.4 %collective-permute-start.5 = (bf16[128,1536]{1,0:T(8,128)(2,1)S(1)}, bf16[128,1536]{1,0:T(8,128)(2,1)S(1)}, u32[]{:S(2)}, u32[]{:S(2)}) collective-permute-start(bf16[128,1536]{1,0:T(8,128)(2,1)S(1)} %bitcast.42), channel_id=1, source_target_pairs={{0,3},{1,0},{2,1},{3,2},{4,7},{5,4},{6,5},{7,6},{8,11},{9,8},{10,9... | collective-permute-start | bytes 1179656 | tf_op jit(solution)/shard_map/ppermute | solution.py:20
  36.6 3.6 %collective-permute-start.2 = (bf16[264,384]{1,0:T(8,128)(2,1)S(1)}, bf16[264,384]{1,0:T(8,128)(2,1)S(1)}, u32[]{:S(2)}, u32[]{:S(2)}) collective-permute-start(bf16[264,384]{1,0:T(8,128)(2,1)S(1)} %get-tuple-element.49), channel_id=1, source_target_pairs={{0,3},{1,0},{2,1},{3,2},{4,7},{5,4},{6,5},{7,6},{8,11},{9,8},{10,9... | collective-permute-start | bytes 608264 | tf_op jit(solution)/shard_map/ppermute | solution.py:20
  40.2 18.5 %collective-permute-done.5.refs_4_ = bf16[128,1536]{1,0:T(8,128)(2,1)S(1)} collective-permute-done((bf16[128,1536]{1,0:T(8,128)(2,1)S(1)}, bf16[128,1536]{1,0:T(8,128)(2,1)S(1)}, u32[]{:S(2)}, u32[]{:S(2)}) %collective-permute-start.5) | collective-permute-done | bytes 393248 | tf_op jit(solution)/shard_map/ppermute | solution.py:20
  58.7 3.3 %collective-permute-start.6 = (bf16[64,1536]{1,0:T(8,128)(2,1)S(1)}, bf16[64,1536]{1,0:T(8,128)(2,1)S(1)}, u32[]{:S(2)}, u32[]{:S(2)}) collective-permute-start(bf16[64,1536]{1,0:T(8,128)(2,1)S(1)} %slice.17), channel_id=1, source_target_pairs={{0,3},{1,0},{2,1},{3,2},{4,7},{5,4},{6,5},{7,6},{8,11},{9,8},{10,9... | collective-permute-start | bytes 589832 | tf_op jit(solution)/shard_map/ppermute | solution.py:20
  73.0 3.6 %collective-permute-start.8 = (bf16[256,384]{1,0:T(8,128)(2,1)S(1)}, bf16[256,384]{1,0:T(8,128)(2,1)S(1)}, u32[]{:S(2)}, u32[]{:S(2)}) collective-permute-start(bf16[256,384]{1,0:T(8,128)(2,1)S(1)} %get-tuple-element.42), channel_id=1, source_target_pairs={{0,2},{1,3},{2,0},{3,1},{4,6},{5,7},{6,4},{7,5},{8,10},{9,11},{10,... | collective-permute-start | bytes 589832 | tf_op jit(solution)/shard_map/ppermute | solution.py:20
  79.2 5.4 %project.1 = (bf16[1536,512]{1,0:T(8,128)(2,1)S(1)}, bf16[512,1152]{1,0:T(8,128)(2,1)S(1)}) custom-call(bf16[128,1536]{1,0:T(8,128)(2,1)} %bitcast.40, bf16[128,1536]{1,0:T(8,128)(2,1)} %copy-done.10, bf16[64,1536]{1,0:T(8,128)(2,1)} %copy-done.19, bf16[64,1536]{1,0:T(8,128)(2,1)} %copy-done.18, bf16[128,1536]{1,0:T(8,128)(2,1)} %copy-done.9, ...), custom_call_target="tpu_custom_call" | custom-call | tf_op jit(solution)/shard_map/project/pallas_call | solution.py:136
  85.4 7.6 %attention_weights.1.refs_0_ = bf16[3,512,1536]{2,1,0:T(8,128)(2,1)S(1)} custom-call(bf16[264,384]{1,0:T(8,128)(2,1)} %get-tuple-element.50.refs_0_.refs_6_, bf16[264,384]{1,0:T(8,128)(2,1)} %copy-done.3, bf16[264,384]{1,0:T(8,128)(2,1)} %copy-done.4, bf16[264,384]{1,0:T(8,128)(2,1)} %copy-done.2, ...), custom_call_target="tpu_custom_call" | custom-call | tf_op jit(solution)/shard_map/attention_weights/pallas_call | solution.py:184
  95.4 3.6 %attention_mix.1 = (bf16[128,384]{1,0:T(8,128)(2,1)}, bf16[128,384]{1,0:T(8,128)(2,1)}, bf16[128,384]{1,0:T(8,128)(2,1)}, bf16[128,384]{1,0:T(8,128)(2,1)}) custom-call(bf16[3,512,1536]{2,1,0:T(8,128)(2,1)S(1)} %attention_weights.1.refs_0_, bf16[256,384]{1,0:T(8,128)(2,1)} %get-tuple-element.41.refs_1_.refs_10_, bf16[256,384]{1,0:T(8,128)(2,1)} %copy-done.6, ...), custom_call_target="tpu_custom_call" | custom-call | tf_op jit(solution)/shard_map/attention_mix/pallas_call | solution.py:212
  101.0 6.1 %collective-permute-start.11 = (bf16[128,384]{1,0:T(8,128)(2,1)}, bf16[128,384]{1,0:T(8,128)(2,1)S(1)}, u32[]{:S(2)}, u32[]{:S(2)}) collective-permute-start(bf16[128,384]{1,0:T(8,128)(2,1)} %get-tuple-element.24.refs_10_), channel_id=1, source_target_pairs={{0,2},{1,3},{2,0},{3,1},{4,6},{5,7},{6,4},{7,5},{8,10},{9,11},{10,... | collective-permute-start | bytes 294920 | tf_op jit(solution)/shard_map/ppermute | solution.py:20
  109.4 5.8 %collective-permute-done.12.refs_3_ = bf16[128,384]{1,0:T(8,128)(2,1)S(1)} collective-permute-done((bf16[128,384]{1,0:T(8,128)(2,1)}, bf16[128,384]{1,0:T(8,128)(2,1)S(1)}, u32[]{:S(2)}, u32[]{:S(2)}) %collective-permute-start.12) | collective-permute-done | bytes 98336 | tf_op jit(solution)/shard_map/ppermute | solution.py:20
  115.9 9.7 %middle.1 = (bf16[128,1536]{1,0:T(8,128)(2,1)}, bf16[128,1536]{1,0:T(8,128)(2,1)}, bf16[136,384]{1,0:T(8,128)(2,1)S(1)}, bf16[136,384]{1,0:T(8,128)(2,1)S(1)}, b...) custom-call(bf16[128,384]{1,0:T(8,128)(2,1)} %get-tuple-element.22.refs_0_.refs_8_, ...), custom_call_target="tpu_custom_call" | custom-call | tf_op jit(solution)/shard_map/middle/pallas_call | solution.py:298
  129.2 3.1 %collective-permute-start.22 = (bf16[128,1536]{1,0:T(8,128)(2,1)}, bf16[128,1536]{1,0:T(8,128)(2,1)S(1)}, u32[]{:S(2)}, u32[]{:S(2)}) collective-permute-start(bf16[128,1536]{1,0:T(8,128)(2,1)} %get-tuple-element.36.refs_4_), channel_id=1, source_target_pairs={{0,2},{1,3},{2,0},{3,1},{4,6},{5,7},{6,4},{7,5},{8,10},{9,11},{10,... | collective-permute-start | bytes 1179656 | tf_op jit(solution)/shard_map/ppermute | solution.py:20
  134.6 3.6 %collective-permute-start.18 = (bf16[136,384]{1,0:T(8,128)(2,1)S(1)}, bf16[136,384]{1,0:T(8,128)(2,1)S(1)}, u32[]{:S(2)}, u32[]{:S(2)}) collective-permute-start(bf16[136,384]{1,0:T(8,128)(2,1)S(1)} %get-tuple-element.31), channel_id=1, source_target_pairs={{0,3},{1,0},{2,1},{3,2},{4,7},{5,4},{6,5},{7,6},{8,11},{9,8},{10,9... | collective-permute-start | bytes 313352 | tf_op jit(solution)/shard_map/ppermute | solution.py:20
  138.2 30.1 %collective-permute-done.17.refs_4_.refs_2_ = bf16[136,384]{1,0:T(8,128)(2,1)S(1)} collective-permute-done((bf16[136,384]{1,0:T(8,128)(2,1)S(1)}, bf16[136,384]{1,0:T(8,128)(2,1)S(1)}, u32[]{:S(2)}, u32[]{:S(2)}) %collective-permute-start.17) | collective-permute-done | bytes 104480 | tf_op jit(solution)/shard_map/ppermute | solution.py:20
  168.3 5.0 %backward.3 = (bf16[768,384]{1,0:T(8,128)(2,1)}, bf16[768,384]{1,0:T(8,128)(2,1)}) custom-call(bf16[3,512,1536]{2,1,0:T(8,128)(2,1)S(1)} %bitcast.37, bf16[1536,512]{1,0:T(8,128)(2,1)S(1)} %get-tuple-element.27.refs_1_, bf16[136,384]{1,0:T(8,128)(2,1)S(1)} %get-tuple-element.28.refs_2_.refs_0_, bf16[136,384]{1,0:T(8,128)(2,1)S(1)} %collective-permute-done.16.refs_3_.refs_1_, ...), custom_call_target="tpu_custom_call" | custom-call | tf_op jit(solution)/shard_map/backward/pallas_call | solution.py:376
  175.8 4.2 %out_gradient.1 = (bf16[768,384]{1,0:T(8,128)(2,1)}, bf16[768,384]{1,0:T(8,128)(2,1)}) custom-call(bf16[136,384]{1,0:T(8,128)(2,1)S(1)} %get-tuple-element.28.refs_2_.refs_0_, bf16[136,384]{1,0:T(8,128)(2,1)S(1)} %collective-permute-done.16.refs_3_.refs_1_, bf16[136,384]{1,0:T(8,128)(2,1)S(1)} %collective-permute-done.17.refs_4_.refs_2_, ...), custom_call_target="tpu_custom_call" | custom-call | tf_op jit(solution)/shard_map/out_gradient/pallas_call | solution.py:413
  183.5 15.3 %all-to-all-start.1 = ((bf16[32,24,768]{2,1,0:T(8,128)(2,1)}), bf16[32,24,768]{2,1,0:T(8,128)(2,1)}, u32[]{:S(2)}, u32[]{:S(2)}) async-start(bf16[32,24,768]{2,1,0:T(8,128)(2,1)} %bitcast.39), calls=%async_computation.1 | async-start | bytes 2359296 | tf_op jit(solution)/shard_map/all_to_all | solution.py:431
  201.1 8.0 %backward.2 = (bf16[768,768]{1,0:T(8,128)(2,1)}, bf16[768,768]{1,0:T(8,128)(2,1)}) custom-call(bf16[3,512,1536]{2,1,0:T(8,128)(2,1)S(1)} %copy-done.1, bf16[1536,512]{1,0:T(8,128)(2,1)S(1)} %get-tuple-element.27.refs_1_, bf16[136,384]{1,0:T(8,128)(2,1)S(1)} %get-tuple-element.28.refs_2_.refs_0_, ...), custom_call_target="tpu_custom_call" | custom-call | tf_op jit(solution)/shard_map/backward/pallas_call | solution.py:376
  217.4 5.4 %all-to-all-start = ((bf16[32,24,768]{2,1,0:T(8,128)(2,1)}), bf16[32,24,768]{2,1,0:T(8,128)(2,1)S(1)}, u32[]{:S(2)}, u32[]{:S(2)}) async-start(bf16[32,24,768]{2,1,0:T(8,128)(2,1)} %bitcast.17), calls=%async_computation | async-start | bytes 2359296 | tf_op jit(solution)/shard_map/all_to_all | solution.py:431
  224.9 16.3 %all-to-all-done = bf16[32,24,768]{2,1,0:T(8,128)(2,1)S(1)} async-done(((bf16[32,24,768]{2,1,0:T(8,128)(2,1)}), bf16[32,24,768]{2,1,0:T(8,128)(2,1)S(1)}, u32[]{:S(2)}, u32[]{:S(2)}) %all-to-all-start) | async-done | bytes 1179680 | tf_op jit(solution)/shard_map/all_to_all | solution.py:431
  (128 shorter events, 53.5 us)
Async XLA Ops:
  7.2 108.0 %all-gather.2.cloned.1.call-start = ((), (), s32[]{:S(2)}) async-start(), calls=%async_computation.2 | async-start | bytes 14598144 | tf_op jit(solution)/shard_map/all_gather | solution.py:466
  8.7 11.3 %collective-permute-start.15 = (bf16[3,48,384]{2,1,0:T(8,128)(2,1)}, bf16[3,48,384]{2,1,0:T(8,128)(2,1)S(1)}, u32[]{:S(2)}, u32[]{:S(2)}) collective-permute-start(bf16[3,48,384]{2,1,0:T(8,128)(2,1)} %weight_slices.1.refs_0_), channel_id=1, source_target_pairs={{0,1},{1,2},{2,3},{3,0},{4,5},{5,6},{6,7},{7,4},{8,9},{9,10},{10,1... | collective-permute-start | bytes 331784 | tf_op jit(solution)/shard_map/ppermute | solution.py:20
  12.5 12.6 %collective-permute-start.14 = (bf16[3,48,384]{2,1,0:T(8,128)(2,1)}, bf16[3,48,384]{2,1,0:T(8,128)(2,1)S(1)}, u32[]{:S(2)}, u32[]{:S(2)}) collective-permute-start(bf16[3,48,384]{2,1,0:T(8,128)(2,1)} %weight_slices.1.refs_0_), channel_id=1, source_target_pairs={{0,2},{1,3},{2,0},{3,1},{4,6},{5,7},{6,4},{7,5},{8,10},{9,11},{10,... | collective-permute-start | bytes 331784 | tf_op jit(solution)/shard_map/ppermute | solution.py:20
  17.6 11.4 %collective-permute-start.13 = (bf16[3,48,384]{2,1,0:T(8,128)(2,1)}, bf16[3,48,384]{2,1,0:T(8,128)(2,1)S(1)}, u32[]{:S(2)}, u32[]{:S(2)}) collective-permute-start(bf16[3,48,384]{2,1,0:T(8,128)(2,1)} %weight_slices.1.refs_0_), channel_id=1, source_target_pairs={{0,3},{1,0},{2,1},{3,2},{4,7},{5,4},{6,5},{7,6},{8,11},{9,8},{10,9... | collective-permute-start | bytes 331784 | tf_op jit(solution)/shard_map/ppermute | solution.py:20
  31.5 27.1 %collective-permute-start.5 = (bf16[128,1536]{1,0:T(8,128)(2,1)S(1)}, bf16[128,1536]{1,0:T(8,128)(2,1)S(1)}, u32[]{:S(2)}, u32[]{:S(2)}) collective-permute-start(bf16[128,1536]{1,0:T(8,128)(2,1)S(1)} %bitcast.42), channel_id=1, source_target_pairs={{0,3},{1,0},{2,1},{3,2},{4,7},{5,4},{6,5},{7,6},{8,11},{9,8},{10,9... | collective-permute-start | bytes 1179656 | tf_op jit(solution)/shard_map/ppermute | solution.py:20
  34.9 27.1 %collective-permute-start.3 = (bf16[128,1536]{1,0:T(8,128)(2,1)S(1)}, bf16[128,1536]{1,0:T(8,128)(2,1)S(1)}, u32[]{:S(2)}, u32[]{:S(2)}) collective-permute-start(bf16[128,1536]{1,0:T(8,128)(2,1)S(1)} %bitcast.43), channel_id=1, source_target_pairs={{0,1},{1,2},{2,3},{3,0},{4,5},{5,6},{6,7},{7,4},{8,9},{9,10},{10,1... | collective-permute-start | bytes 1179656 | tf_op jit(solution)/shard_map/ppermute | solution.py:20
  36.6 32.0 %collective-permute-start.2 = (bf16[264,384]{1,0:T(8,128)(2,1)S(1)}, bf16[264,384]{1,0:T(8,128)(2,1)S(1)}, u32[]{:S(2)}, u32[]{:S(2)}) collective-permute-start(bf16[264,384]{1,0:T(8,128)(2,1)S(1)} %get-tuple-element.49), channel_id=1, source_target_pairs={{0,3},{1,0},{2,1},{3,2},{4,7},{5,4},{6,5},{7,6},{8,11},{9,8},{10,9... | collective-permute-start | bytes 608264 | tf_op jit(solution)/shard_map/ppermute | solution.py:20
  58.7 12.4 %collective-permute-start.6 = (bf16[64,1536]{1,0:T(8,128)(2,1)S(1)}, bf16[64,1536]{1,0:T(8,128)(2,1)S(1)}, u32[]{:S(2)}, u32[]{:S(2)}) collective-permute-start(bf16[64,1536]{1,0:T(8,128)(2,1)S(1)} %slice.17), channel_id=1, source_target_pairs={{0,3},{1,0},{2,1},{3,2},{4,7},{5,4},{6,5},{7,6},{8,11},{9,8},{10,9... | collective-permute-start | bytes 589832 | tf_op jit(solution)/shard_map/ppermute | solution.py:20
  62.1 10.9 %collective-permute-start.4 = (bf16[64,1536]{1,0:T(8,128)(2,1)S(1)}, bf16[64,1536]{1,0:T(8,128)(2,1)S(1)}, u32[]{:S(2)}, u32[]{:S(2)}) collective-permute-start(bf16[64,1536]{1,0:T(8,128)(2,1)S(1)} %slice.16), channel_id=1, source_target_pairs={{0,1},{1,2},{2,3},{3,0},{4,5},{5,6},{6,7},{7,4},{8,9},{9,10},{10,1... | collective-permute-start | bytes 589832 | tf_op jit(solution)/shard_map/ppermute | solution.py:20
  62.2 22.5 %collective-permute-start = (bf16[264,384]{1,0:T(8,128)(2,1)S(1)}, bf16[264,384]{1,0:T(8,128)(2,1)S(1)}, u32[]{:S(2)}, u32[]{:S(2)}) collective-permute-start(bf16[264,384]{1,0:T(8,128)(2,1)S(1)} %get-tuple-element.51), channel_id=1, source_target_pairs={{0,1},{1,2},{2,3},{3,0},{4,5},{5,6},{6,7},{7,4},{8,9},{9,10},{10,1... | collective-permute-start | bytes 608264 | tf_op jit(solution)/shard_map/ppermute | solution.py:20
  65.2 19.5 %collective-permute-start.1 = (bf16[264,384]{1,0:T(8,128)(2,1)S(1)}, bf16[264,384]{1,0:T(8,128)(2,1)S(1)}, u32[]{:S(2)}, u32[]{:S(2)}) collective-permute-start(bf16[264,384]{1,0:T(8,128)(2,1)S(1)} %get-tuple-element.52), channel_id=1, source_target_pairs={{0,2},{1,3},{2,0},{3,1},{4,6},{5,7},{6,4},{7,5},{8,10},{9,11},{10,... | collective-permute-start | bytes 608264 | tf_op jit(solution)/shard_map/ppermute | solution.py:20
  68.6 24.5 %collective-permute-start.9 = (bf16[256,384]{1,0:T(8,128)(2,1)S(1)}, bf16[256,384]{1,0:T(8,128)(2,1)S(1)}, u32[]{:S(2)}, u32[]{:S(2)}) collective-permute-start(bf16[256,384]{1,0:T(8,128)(2,1)S(1)} %get-tuple-element.39), channel_id=1, source_target_pairs={{0,3},{1,0},{2,1},{3,2},{4,7},{5,4},{6,5},{7,6},{8,11},{9,8},{10,9... | collective-permute-start | bytes 589832 | tf_op jit(solution)/shard_map/ppermute | solution.py:20
  71.1 21.9 %collective-permute-start.7 = (bf16[256,384]{1,0:T(8,128)(2,1)S(1)}, bf16[256,384]{1,0:T(8,128)(2,1)S(1)}, u32[]{:S(2)}, u32[]{:S(2)}) collective-permute-start(bf16[256,384]{1,0:T(8,128)(2,1)S(1)} %get-tuple-element.40), channel_id=1, source_target_pairs={{0,1},{1,2},{2,3},{3,0},{4,5},{5,6},{6,7},{7,4},{8,9},{9,10},{10,1... | collective-permute-start | bytes 589832 | tf_op jit(solution)/shard_map/ppermute | solution.py:20
  73.0 21.5 %collective-permute-start.8 = (bf16[256,384]{1,0:T(8,128)(2,1)S(1)}, bf16[256,384]{1,0:T(8,128)(2,1)S(1)}, u32[]{:S(2)}, u32[]{:S(2)}) collective-permute-start(bf16[256,384]{1,0:T(8,128)(2,1)S(1)} %get-tuple-element.42), channel_id=1, source_target_pairs={{0,2},{1,3},{2,0},{3,1},{4,6},{5,7},{6,4},{7,5},{8,10},{9,11},{10,... | collective-permute-start | bytes 589832 | tf_op jit(solution)/shard_map/ppermute | solution.py:20
  101.0 8.5 %collective-permute-start.11 = (bf16[128,384]{1,0:T(8,128)(2,1)}, bf16[128,384]{1,0:T(8,128)(2,1)S(1)}, u32[]{:S(2)}, u32[]{:S(2)}) collective-permute-start(bf16[128,384]{1,0:T(8,128)(2,1)} %get-tuple-element.24.refs_10_), channel_id=1, source_target_pairs={{0,2},{1,3},{2,0},{3,1},{4,6},{5,7},{6,4},{7,5},{8,10},{9,11},{10,... | collective-permute-start | bytes 294920 | tf_op jit(solution)/shard_map/ppermute | solution.py:20
  107.0 8.2 %collective-permute-start.12 = (bf16[128,384]{1,0:T(8,128)(2,1)}, bf16[128,384]{1,0:T(8,128)(2,1)S(1)}, u32[]{:S(2)}, u32[]{:S(2)}) collective-permute-start(bf16[128,384]{1,0:T(8,128)(2,1)} %get-tuple-element.25.refs_11_), channel_id=1, source_target_pairs={{0,1},{1,2},{2,3},{3,0},{4,5},{5,6},{6,7},{7,4},{8,9},{9,10},{10,1... | collective-permute-start | bytes 294920 | tf_op jit(solution)/shard_map/ppermute | solution.py:20
  125.6 9.0 %collective-permute-start.16 = (bf16[136,384]{1,0:T(8,128)(2,1)S(1)}, bf16[136,384]{1,0:T(8,128)(2,1)S(1)}, u32[]{:S(2)}, u32[]{:S(2)}) collective-permute-start(bf16[136,384]{1,0:T(8,128)(2,1)S(1)} %get-tuple-element.29), channel_id=1, source_target_pairs={{0,1},{1,2},{2,3},{3,0},{4,5},{5,6},{6,7},{7,4},{8,9},{9,10},{10,1... | collective-permute-start | bytes 313352 | tf_op jit(solution)/shard_map/ppermute | solution.py:20
  126.5 47.7 %collective-permute-start.23 = (bf16[128,1536]{1,0:T(8,128)(2,1)}, bf16[128,1536]{1,0:T(8,128)(2,1)S(1)}, u32[]{:S(2)}, u32[]{:S(2)}) collective-permute-start(bf16[128,1536]{1,0:T(8,128)(2,1)} %get-tuple-element.36.refs_4_), channel_id=1, source_target_pairs={{0,3},{1,0},{2,1},{3,2},{4,7},{5,4},{6,5},{7,6},{8,11},{9,8},{10,9... | collective-permute-start | bytes 1179656 | tf_op jit(solution)/shard_map/ppermute | solution.py:20
  129.2 44.9 %collective-permute-start.22 = (bf16[128,1536]{1,0:T(8,128)(2,1)}, bf16[128,1536]{1,0:T(8,128)(2,1)S(1)}, u32[]{:S(2)}, u32[]{:S(2)}) collective-permute-start(bf16[128,1536]{1,0:T(8,128)(2,1)} %get-tuple-element.36.refs_4_), channel_id=1, source_target_pairs={{0,2},{1,3},{2,0},{3,1},{4,6},{5,7},{6,4},{7,5},{8,10},{9,11},{10,... | collective-permute-start | bytes 1179656 | tf_op jit(solution)/shard_map/ppermute | solution.py:20
  132.4 41.8 %collective-permute-start.21 = (bf16[128,1536]{1,0:T(8,128)(2,1)}, bf16[128,1536]{1,0:T(8,128)(2,1)S(1)}, u32[]{:S(2)}, u32[]{:S(2)}) collective-permute-start(bf16[128,1536]{1,0:T(8,128)(2,1)} %get-tuple-element.36.refs_4_), channel_id=1, source_target_pairs={{0,1},{1,2},{2,3},{3,0},{4,5},{5,6},{6,7},{7,4},{8,9},{9,10},{10,1... | collective-permute-start | bytes 1179656 | tf_op jit(solution)/shard_map/ppermute | solution.py:20
  132.4 35.9 %collective-permute-start.17 = (bf16[136,384]{1,0:T(8,128)(2,1)S(1)}, bf16[136,384]{1,0:T(8,128)(2,1)S(1)}, u32[]{:S(2)}, u32[]{:S(2)}) collective-permute-start(bf16[136,384]{1,0:T(8,128)(2,1)S(1)} %get-tuple-element.30), channel_id=1, source_target_pairs={{0,2},{1,3},{2,0},{3,1},{4,6},{5,7},{6,4},{7,5},{8,10},{9,11},{10,... | collective-permute-start | bytes 313352 | tf_op jit(solution)/shard_map/ppermute | solution.py:20
  134.6 33.7 %collective-permute-start.18 = (bf16[136,384]{1,0:T(8,128)(2,1)S(1)}, bf16[136,384]{1,0:T(8,128)(2,1)S(1)}, u32[]{:S(2)}, u32[]{:S(2)}) collective-permute-start(bf16[136,384]{1,0:T(8,128)(2,1)S(1)} %get-tuple-element.31), channel_id=1, source_target_pairs={{0,3},{1,0},{2,1},{3,2},{4,7},{5,4},{6,5},{7,6},{8,11},{9,8},{10,9... | collective-permute-start | bytes 313352 | tf_op jit(solution)/shard_map/ppermute | solution.py:20
  183.5 33.9 %all-to-all-start.1 = ((bf16[32,24,768]{2,1,0:T(8,128)(2,1)}), bf16[32,24,768]{2,1,0:T(8,128)(2,1)}, u32[]{:S(2)}, u32[]{:S(2)}) async-start(bf16[32,24,768]{2,1,0:T(8,128)(2,1)} %bitcast.39), calls=%async_computation.1 | async-start | bytes 2359296 | tf_op jit(solution)/shard_map/all_to_all | solution.py:431
  217.4 23.8 %all-to-all-start = ((bf16[32,24,768]{2,1,0:T(8,128)(2,1)}), bf16[32,24,768]{2,1,0:T(8,128)(2,1)S(1)}, u32[]{:S(2)}, u32[]{:S(2)}) async-start(bf16[32,24,768]{2,1,0:T(8,128)(2,1)} %bitcast.17), calls=%async_computation | async-start | bytes 2359296 | tf_op jit(solution)/shard_map/all_to_all | solution.py:431
  (36 other events, 469.0 us)
Sparse Core Ops, SparseCore 0:
  31.7 71.7 all-gather.1

commit v2 on v1

--- a/solution.py
+++ b/solution.py
@@ -156,10 +156,8 @@
         for p in parts
     ]
     step = 128
-
-    @pl.loop(0, q_ref.shape[0] // step)
-    def _(r):
-        rows = pl.ds(pl.multiple_of(r * step, step), step)
+    for r in range(q_ref.shape[0] // step):
+        rows = slice(r * step, (r + 1) * step)
         query = q_ref[rows]
         scores = [dot(query, k, NT) * factor for k in keys]
         for n in range(SEQ):
@@ -245,19 +243,18 @@
     outs, (out_w, held, sems) = refs[8 : 8 + SEQ], refs[8 + SEQ :]
     width = parts[0].shape[1]
 
-    @pl.loop(0, SEQ)
-    def _(j):
+    for k in range(SEQ):
+        j = place_in_seq(k)
         for c in range(SEQ):
             pltpu.make_async_copy(
                 w_ref.at[0, :, c, :, pl.ds(pl.multiple_of(j * width, 128), width)],
                 out_w.at[j, :, :, c * width : (c + 1) * width],
-                sems.at[0],
+                sems.at[k],
             ).start()
-
-    copies = [pltpu.make_async_copy(out_w, out_w, sems.at[0])]
-    for n in (1, 2):
-        copies.append(pltpu.make_async_copy(w_ref.at[n], held.at[n - 1], sems.at[n]))
-        copies[n].start()
+    copies = [pltpu.make_async_copy(out_w.at[k], out_w.at[k], sems.at[k]) for k in range(SEQ)]
+    for n in range(2):
+        copies.append(pltpu.make_async_copy(w_ref.at[n + 1], held.at[n], sems.at[SEQ + n]))
+        copies[-1].start()
 
     def block(k):
         rows = out_w[place_in_seq(k)]
@@ -266,6 +263,7 @@
     copies[0].wait()
     update = dot(parts[0][...], block(0))
     for k in range(1, SEQ):
+        copies[k].wait()
         update += dot(parts[k][...], block(k))
     clean = (latents_ref[...].astype(jnp.float32) + update).astype(jnp.bfloat16)
     clean_ref[...] = clean
@@ -279,10 +277,10 @@
     gain_shape = (clean.shape[1], clean.shape[1])
     real_in = (scaled * real_gain_ref[...]).astype(jnp.bfloat16)
     fake_in = (scaled * fake_gain_ref[...]).astype(jnp.bfloat16)
-    copies[1].wait()
+    copies[SEQ].wait()
     pred_real = noisy + dot(real_in, held[0].reshape(gain_shape))
     total = jnp.sum(jnp.abs(clean_f - pred_real), axis=(0, 1), keepdims=True)
-    copies[2].wait()
+    copies[SEQ + 1].wait()
     pred_fake = noisy + dot(fake_in, held[1].reshape(gain_shape))
     gap = (pred_fake - pred_real).astype(jnp.bfloat16)
     gap_ref[...] = gap
@@ -304,7 +302,7 @@
         scratch_shapes=[
             pltpu.VMEM((SEQ, whole.shape[1], *whole.shape[3:]), jnp.bfloat16),
             pltpu.VMEM((2, *whole.shape[1:]), jnp.bfloat16),
-            pltpu.SemaphoreType.DMA((3,)),
+            pltpu.SemaphoreType.DMA((SEQ + 2,)),
         ],
         compiler_params=within(30),
         name="middle",
@@ -421,9 +419,12 @@
     )(*near(*grads), *far(*gaps, *mixed))
 
 
-def chip_sum(send, keep):
-    arrived = lax.ppermute(send, "dp", [(i, i ^ 1) for i in range(PARTS)])
-    return (keep.astype(jnp.float32) + arrived.astype(jnp.float32)).astype(jnp.bfloat16)
+def swapped(x):
+    return lax.ppermute(x, "dp", [(n, n ^ 1) for n in range(PARTS)])
+
+
+def added(a, b):
+    return (a.astype(jnp.float32) + b.astype(jnp.float32)).astype(jnp.bfloat16)
 
 
 def summed_over_chips(x):
@@ -496,12 +497,14 @@
         halves = backward(
             heads[0], len(heads), weights, turned, grads, key_parts, value_parts, packed
         )
-        sums.append(chip_sum(*halves))
+        sums.append((swapped(halves[0]), halves[1]))
     halves = out_gradient(grads, gaps, mixed)
-    outg = chip_sum(*halves)
-    share_a = summed_over_chips(sums[0])
-    share_b = summed_over_chips(jnp.concatenate([sums[1], outg], axis=1))
-    rest = sums[1].shape[1]
+    sums.append((swapped(halves[0]), halves[1]))
+    share_a = summed_over_chips(added(*sums[0]))
+    share_b = summed_over_chips(
+        added(*(jnp.concatenate([p, q], axis=1) for p, q in zip(sums[1], sums[2])))
+    )
+    rest = sums[1][0].shape[1]
     qkv_share = jnp.concatenate([share_a, share_b[:, :rest]], axis=1)
     return (clean[None], qkv_share, share_b[:, rest:].T)
 

time: 250 us -> 256 us (1.024)
  waiting for transfers between devices: 91.3 us -> 98.2 us
    ppermute x22, waiting for transfers between devices: 67.7 us -> 74.5 us  [shifted(): return lax.ppermute(x, 'seq', [(i, (i + by) % SEQ) for i in range(SEQ)])]
    unnamed x66 -> x64, local copies, waits for them, and re-layouts: 6.3 us -> 6.11 us
  transfers between devices with their start and end apart: 28 -> 28, of which waited for: 12 -> 14; matrix products, arithmetic and copies ran while one was open for 3% -> 3% of each run, Pallas kernels for 14% -> 12%
where the time goes in v2:
time: 256 us; the launch traced here: 255 us
  waiting for transfers between devices  98.2 us (38%)
  starting transfers between devices  78.1 us (31%)
  Pallas kernels  44.4 us (17%)
  between operations  15.8 us (6%)
  local copies, waits for them, and re-layouts  10 us (4%)
  other arithmetic  8.26 us (3%)
    ppermute x22, waiting for transfers between devices, shifted(): return lax.ppermute(x, 'seq', [(i, (i + by) % SEQ) for i in range(SEQ)])  74.5 us
    ppermute x22, starting transfers between devices, shifted(): return lax.ppermute(x, 'seq', [(i, (i + by) % SEQ) for i in range(SEQ)])  54.4 us
    all_to_all x2, starting transfers between devices, summed_over_chips(): lax.all_to_all(pieces, 'dp', split_axis=0, concat_axis=0, tiled=True, axi...  22.8 us
    all_to_all x2, waiting for transfers between devices, summed_over_chips(): lax.all_to_all(pieces, 'dp', split_axis=0, concat_axis=0, tiled=True, axi...  18.8 us
    pallas_call x2, Pallas kernels, backward(): pl.pallas_call(backward_kernel, grid=(heads,), in_specs=[pl.BlockSpec((1,...  13 us
    pallas_call x1, Pallas kernels, middle(): pl.pallas_call(middle_kernel, in_specs=[VMEM] * (SEQ + 5) + [ANY], out_sp...  9.74 us
    unnamed x64, local copies, waits for them, and re-layouts  6.11 us
    pallas_call x1, Pallas kernels, project(): pl.pallas_call(project_kernel, in_specs=[VMEM] * (len(parts) + 2), out_sp...  5.38 us
  transfers between devices with their start and end apart: 28, of which 14 were waited for; matrix products, arithmetic and copies ran while one was open for 3% of the time, Pallas kernels for 12%

profile of v2, /device:TPU:1, one launch (start us, length us, event | category | flops | bytes accessed | tf_op | source)
XLA Modules:
  0.0 254.9 jit_solution(15764869315133432245)
XLA Ops:
  8.7 3.8 %collective-permute-start.15 = (bf16[3,48,384]{2,1,0:T(8,128)(2,1)}, bf16[3,48,384]{2,1,0:T(8,128)(2,1)S(1)}, u32[]{:S(2)}, u32[]{:S(2)}) collective-permute-start(bf16[3,48,384]{2,1,0:T(8,128)(2,1)} %weight_slices.1.refs_0_), channel_id=1, source_target_pairs={{0,1},{1,2},{2,3},{3,0},{4,5},{5,6},{6,7},{7,4},{8,9},{9,10},{10,1... | collective-permute-start | bytes 331784 | tf_op jit(solution)/shard_map/ppermute | solution.py:20
  12.5 5.1 %collective-permute-start.14 = (bf16[3,48,384]{2,1,0:T(8,128)(2,1)}, bf16[3,48,384]{2,1,0:T(8,128)(2,1)S(1)}, u32[]{:S(2)}, u32[]{:S(2)}) collective-permute-start(bf16[3,48,384]{2,1,0:T(8,128)(2,1)} %weight_slices.1.refs_0_), channel_id=1, source_target_pairs={{0,2},{1,3},{2,0},{3,1},{4,6},{5,7},{6,4},{7,5},{8,10},{9,11},{10,... | collective-permute-start | bytes 331784 | tf_op jit(solution)/shard_map/ppermute | solution.py:20
  20.0 5.1 %collective-permute-done.14.refs_2_ = bf16[3,48,384]{2,1,0:T(8,128)(2,1)S(1)} collective-permute-done((bf16[3,48,384]{2,1,0:T(8,128)(2,1)}, bf16[3,48,384]{2,1,0:T(8,128)(2,1)S(1)}, u32[]{:S(2)}, u32[]{:S(2)}) %collective-permute-start.14) | collective-permute-done | bytes 110624 | tf_op jit(solution)/shard_map/ppermute | solution.py:20
  25.1 3.9 %collective-permute-done.13.refs_1_ = bf16[3,48,384]{2,1,0:T(8,128)(2,1)S(1)} collective-permute-done((bf16[3,48,384]{2,1,0:T(8,128)(2,1)}, bf16[3,48,384]{2,1,0:T(8,128)(2,1)S(1)}, u32[]{:S(2)}, u32[]{:S(2)}) %collective-permute-start.13) | collective-permute-done | bytes 110624 | tf_op jit(solution)/shard_map/ppermute | solution.py:20
  36.6 3.6 %collective-permute-start.2 = (bf16[264,384]{1,0:T(8,128)(2,1)S(1)}, bf16[264,384]{1,0:T(8,128)(2,1)S(1)}, u32[]{:S(2)}, u32[]{:S(2)}) collective-permute-start(bf16[264,384]{1,0:T(8,128)(2,1)S(1)} %get-tuple-element.49), channel_id=1, source_target_pairs={{0,3},{1,0},{2,1},{3,2},{4,7},{5,4},{6,5},{7,6},{8,11},{9,8},{10,9... | collective-permute-start | bytes 608264 | tf_op jit(solution)/shard_map/ppermute | solution.py:20
  40.2 18.5 %collective-permute-done.5.refs_4_ = bf16[128,1536]{1,0:T(8,128)(2,1)S(1)} collective-permute-done((bf16[128,1536]{1,0:T(8,128)(2,1)S(1)}, bf16[128,1536]{1,0:T(8,128)(2,1)S(1)}, u32[]{:S(2)}, u32[]{:S(2)}) %collective-permute-start.5) | collective-permute-done | bytes 393248 | tf_op jit(solution)/shard_map/ppermute | solution.py:20
  72.9 3.6 %collective-permute-start.8 = (bf16[256,384]{1,0:T(8,128)(2,1)S(1)}, bf16[256,384]{1,0:T(8,128)(2,1)S(1)}, u32[]{:S(2)}, u32[]{:S(2)}) collective-permute-start(bf16[256,384]{1,0:T(8,128)(2,1)S(1)} %get-tuple-element.42), channel_id=1, source_target_pairs={{0,2},{1,3},{2,0},{3,1},{4,6},{5,7},{6,4},{7,5},{8,10},{9,11},{10,... | collective-permute-start | bytes 589832 | tf_op jit(solution)/shard_map/ppermute | solution.py:20
  79.2 5.4 %project.1 = (bf16[1536,512]{1,0:T(8,128)(2,1)S(1)}, bf16[512,1152]{1,0:T(8,128)(2,1)S(1)}) custom-call(bf16[128,1536]{1,0:T(8,128)(2,1)} %bitcast.42, bf16[128,1536]{1,0:T(8,128)(2,1)} %copy-done.10, bf16[64,1536]{1,0:T(8,128)(2,1)} %copy-done.18, bf16[64,1536]{1,0:T(8,128)(2,1)} %copy-done.17, bf16[128,1536]{1,0:T(8,128)(2,1)} %copy-done.9, ...), custom_call_target="tpu_custom_call" | custom-call | tf_op jit(solution)/shard_map/project/pallas_call | solution.py:136
  85.3 5.1 %attention_weights.1.refs_0_ = bf16[3,512,1536]{2,1,0:T(8,128)(2,1)S(1)} custom-call(bf16[264,384]{1,0:T(8,128)(2,1)} %get-tuple-element.50.refs_0_.refs_6_, bf16[264,384]{1,0:T(8,128)(2,1)} %copy-done.3, bf16[264,384]{1,0:T(8,128)(2,1)} %copy-done.4, bf16[264,384]{1,0:T(8,128)(2,1)} %copy-done.2, ...), custom_call_target="tpu_custom_call" | custom-call | tf_op jit(solution)/shard_map/attention_weights/pallas_call | solution.py:182
  90.5 4.1 %collective-permute-done.8.refs_3_.refs_12_ = bf16[256,384]{1,0:T(8,128)(2,1)S(1)} collective-permute-done((bf16[256,384]{1,0:T(8,128)(2,1)S(1)}, bf16[256,384]{1,0:T(8,128)(2,1)S(1)}, u32[]{:S(2)}, u32[]{:S(2)}) %collective-permute-start.8) | collective-permute-done | bytes 196640 | tf_op jit(solution)/shard_map/ppermute | solution.py:20
  95.2 3.7 %attention_mix.1 = (bf16[128,384]{1,0:T(8,128)(2,1)}, bf16[128,384]{1,0:T(8,128)(2,1)}, bf16[128,384]{1,0:T(8,128)(2,1)}, bf16[128,384]{1,0:T(8,128)(2,1)}) custom-call(bf16[3,512,1536]{2,1,0:T(8,128)(2,1)S(1)} %attention_weights.1.refs_0_, bf16[256,384]{1,0:T(8,128)(2,1)} %get-tuple-element.41.refs_1_.refs_10_, bf16[256,384]{1,0:T(8,128)(2,1)} %copy-done.6, ...), custom_call_target="tpu_custom_call" | custom-call | tf_op jit(solution)/shard_map/attention_mix/pallas_call | solution.py:210
  100.4 6.5 %collective-permute-start.11 = (bf16[128,384]{1,0:T(8,128)(2,1)}, bf16[128,384]{1,0:T(8,128)(2,1)S(1)}, u32[]{:S(2)}, u32[]{:S(2)}) collective-permute-start(bf16[128,384]{1,0:T(8,128)(2,1)} %get-tuple-element.24.refs_10_), channel_id=1, source_target_pairs={{0,2},{1,3},{2,0},{3,1},{4,6},{5,7},{6,4},{7,5},{8,10},{9,11},{10,... | collective-permute-start | bytes 294920 | tf_op jit(solution)/shard_map/ppermute | solution.py:20
  109.3 5.0 %collective-permute-done.12.refs_3_ = bf16[128,384]{1,0:T(8,128)(2,1)S(1)} collective-permute-done((bf16[128,384]{1,0:T(8,128)(2,1)}, bf16[128,384]{1,0:T(8,128)(2,1)S(1)}, u32[]{:S(2)}, u32[]{:S(2)}) %collective-permute-start.12) | collective-permute-done | bytes 98336 | tf_op jit(solution)/shard_map/ppermute | solution.py:20
  115.0 9.7 %middle.1 = (bf16[128,1536]{1,0:T(8,128)(2,1)}, bf16[128,1536]{1,0:T(8,128)(2,1)}, bf16[136,384]{1,0:T(8,128)(2,1)S(1)}, bf16[136,384]{1,0:T(8,128)(2,1)S(1)}, b...) custom-call(bf16[128,384]{1,0:T(8,128)(2,1)} %get-tuple-element.22.refs_0_.refs_8_, ...), custom_call_target="tpu_custom_call" | custom-call | tf_op jit(solution)/shard_map/middle/pallas_call | solution.py:296
  126.0 4.5 %collective-permute-start.22 = (bf16[128,1536]{1,0:T(8,128)(2,1)}, bf16[128,1536]{1,0:T(8,128)(2,1)S(1)}, u32[]{:S(2)}, u32[]{:S(2)}) collective-permute-start(bf16[128,1536]{1,0:T(8,128)(2,1)} %get-tuple-element.35.refs_4_), channel_id=1, source_target_pairs={{0,2},{1,3},{2,0},{3,1},{4,6},{5,7},{6,4},{7,5},{8,10},{9,11},{10,... | collective-permute-start | bytes 1179656 | tf_op jit(solution)/shard_map/ppermute | solution.py:20
  131.6 4.5 %collective-permute-start.17 = (bf16[136,384]{1,0:T(8,128)(2,1)S(1)}, bf16[136,384]{1,0:T(8,128)(2,1)S(1)}, u32[]{:S(2)}, u32[]{:S(2)}) collective-permute-start(bf16[136,384]{1,0:T(8,128)(2,1)S(1)} %get-tuple-element.30), channel_id=1, source_target_pairs={{0,2},{1,3},{2,0},{3,1},{4,6},{5,7},{6,4},{7,5},{8,10},{9,11},{10,... | collective-permute-start | bytes 313352 | tf_op jit(solution)/shard_map/ppermute | solution.py:20
  136.1 23.5 %collective-permute-done.16.refs_3_.refs_1_ = bf16[136,384]{1,0:T(8,128)(2,1)S(1)} collective-permute-done((bf16[136,384]{1,0:T(8,128)(2,1)S(1)}, bf16[136,384]{1,0:T(8,128)(2,1)S(1)}, u32[]{:S(2)}, u32[]{:S(2)}) %collective-permute-start.16) | collective-permute-done | bytes 104480 | tf_op jit(solution)/shard_map/ppermute | solution.py:20
  160.0 11.4 %collective-permute-done.18.refs_5_.refs_3_ = bf16[136,384]{1,0:T(8,128)(2,1)S(1)} collective-permute-done((bf16[136,384]{1,0:T(8,128)(2,1)S(1)}, bf16[136,384]{1,0:T(8,128)(2,1)S(1)}, u32[]{:S(2)}, u32[]{:S(2)}) %collective-permute-start.18) | collective-permute-done | bytes 104480 | tf_op jit(solution)/shard_map/ppermute | solution.py:20
  171.4 5.0 %backward.3 = (bf16[768,384]{1,0:T(8,128)(2,1)}, bf16[768,384]{1,0:T(8,128)(2,1)}) custom-call(bf16[3,512,1536]{2,1,0:T(8,128)(2,1)S(1)} %bitcast.40, bf16[1536,512]{1,0:T(8,128)(2,1)S(1)} %get-tuple-element.27.refs_1_, bf16[136,384]{1,0:T(8,128)(2,1)S(1)} %get-tuple-element.28.refs_2_.refs_0_, bf16[136,384]{1,0:T(8,128)(2,1)S(1)} %collective-permute-done.16.refs_3_.refs_1_, ...), custom_call_target="tpu_custom_call" | custom-call | tf_op jit(solution)/shard_map/backward/pallas_call | solution.py:374
  178.6 4.2 %out_gradient.1 = (bf16[768,384]{1,0:T(8,128)(2,1)}, bf16[768,384]{1,0:T(8,128)(2,1)}) custom-call(bf16[136,384]{1,0:T(8,128)(2,1)S(1)} %get-tuple-element.28.refs_2_.refs_0_, bf16[136,384]{1,0:T(8,128)(2,1)S(1)} %collective-permute-done.16.refs_3_.refs_1_, bf16[136,384]{1,0:T(8,128)(2,1)S(1)} %collective-permute-done.17.refs_4_.refs_2_, ...), custom_call_target="tpu_custom_call" | custom-call | tf_op jit(solution)/shard_map/out_gradient/pallas_call | solution.py:411
  187.4 17.3 %all-to-all-start.1 = ((bf16[32,24,768]{2,1,0:T(8,128)(2,1)}), bf16[32,24,768]{2,1,0:T(8,128)(2,1)}, u32[]{:S(2)}, u32[]{:S(2)}) async-start(bf16[32,24,768]{2,1,0:T(8,128)(2,1)} %add_convert_fusion), calls=%async_computation.1 | async-start | bytes 2359296 | tf_op jit(solution)/shard_map/all_to_all | solution.py:432
  207.1 8.0 %backward.2 = (bf16[768,768]{1,0:T(8,128)(2,1)}, bf16[768,768]{1,0:T(8,128)(2,1)}) custom-call(bf16[3,512,1536]{2,1,0:T(8,128)(2,1)S(1)} %copy-done.1, bf16[1536,512]{1,0:T(8,128)(2,1)S(1)} %get-tuple-element.27.refs_1_, bf16[136,384]{1,0:T(8,128)(2,1)S(1)} %get-tuple-element.28.refs_2_.refs_0_, ...), custom_call_target="tpu_custom_call" | custom-call | tf_op jit(solution)/shard_map/backward/pallas_call | solution.py:374
  223.4 5.4 %all-to-all-start = ((bf16[32,24,768]{2,1,0:T(8,128)(2,1)}), bf16[32,24,768]{2,1,0:T(8,128)(2,1)S(1)}, u32[]{:S(2)}, u32[]{:S(2)}) async-start(bf16[32,24,768]{2,1,0:T(8,128)(2,1)} %bitcast.17), calls=%async_computation | async-start | bytes 2359296 | tf_op jit(solution)/shard_map/all_to_all | solution.py:432
  230.9 16.3 %all-to-all-done = bf16[32,24,768]{2,1,0:T(8,128)(2,1)S(1)} async-done(((bf16[32,24,768]{2,1,0:T(8,128)(2,1)}), bf16[32,24,768]{2,1,0:T(8,128)(2,1)S(1)}, u32[]{:S(2)}, u32[]{:S(2)}) %all-to-all-start) | async-done | bytes 1179680 | tf_op jit(solution)/shard_map/all_to_all | solution.py:432
  (124 shorter events, 56.0 us)
Async XLA Ops:
  7.2 107.1 %all-gather.2.cloned.1.call-start = ((), (), s32[]{:S(2)}) async-start(), calls=%async_computation.2 | async-start | bytes 14598144 | tf_op jit(solution)/shard_map/all_gather | solution.py:467
  8.7 11.3 %collective-permute-start.15 = (bf16[3,48,384]{2,1,0:T(8,128)(2,1)}, bf16[3,48,384]{2,1,0:T(8,128)(2,1)S(1)}, u32[]{:S(2)}, u32[]{:S(2)}) collective-permute-start(bf16[3,48,384]{2,1,0:T(8,128)(2,1)} %weight_slices.1.refs_0_), channel_id=1, source_target_pairs={{0,1},{1,2},{2,3},{3,0},{4,5},{5,6},{6,7},{7,4},{8,9},{9,10},{10,1... | collective-permute-start | bytes 331784 | tf_op jit(solution)/shard_map/ppermute | solution.py:20
  12.5 12.6 %collective-permute-start.14 = (bf16[3,48,384]{2,1,0:T(8,128)(2,1)}, bf16[3,48,384]{2,1,0:T(8,128)(2,1)S(1)}, u32[]{:S(2)}, u32[]{:S(2)}) collective-permute-start(bf16[3,48,384]{2,1,0:T(8,128)(2,1)} %weight_slices.1.refs_0_), channel_id=1, source_target_pairs={{0,2},{1,3},{2,0},{3,1},{4,6},{5,7},{6,4},{7,5},{8,10},{9,11},{10,... | collective-permute-start | bytes 331784 | tf_op jit(solution)/shard_map/ppermute | solution.py:20
  17.6 11.4 %collective-permute-start.13 = (bf16[3,48,384]{2,1,0:T(8,128)(2,1)}, bf16[3,48,384]{2,1,0:T(8,128)(2,1)S(1)}, u32[]{:S(2)}, u32[]{:S(2)}) collective-permute-start(bf16[3,48,384]{2,1,0:T(8,128)(2,1)} %weight_slices.1.refs_0_), channel_id=1, source_target_pairs={{0,3},{1,0},{2,1},{3,2},{4,7},{5,4},{6,5},{7,6},{8,11},{9,8},{10,9... | collective-permute-start | bytes 331784 | tf_op jit(solution)/shard_map/ppermute | solution.py:20
  31.6 27.1 %collective-permute-start.5 = (bf16[128,1536]{1,0:T(8,128)(2,1)S(1)}, bf16[128,1536]{1,0:T(8,128)(2,1)S(1)}, u32[]{:S(2)}, u32[]{:S(2)}) collective-permute-start(bf16[128,1536]{1,0:T(8,128)(2,1)S(1)} %bitcast.44), channel_id=1, source_target_pairs={{0,3},{1,0},{2,1},{3,2},{4,7},{5,4},{6,5},{7,6},{8,11},{9,8},{10,9... | collective-permute-start | bytes 1179656 | tf_op jit(solution)/shard_map/ppermute | solution.py:20
  35.0 27.1 %collective-permute-start.3 = (bf16[128,1536]{1,0:T(8,128)(2,1)S(1)}, bf16[128,1536]{1,0:T(8,128)(2,1)S(1)}, u32[]{:S(2)}, u32[]{:S(2)}) collective-permute-start(bf16[128,1536]{1,0:T(8,128)(2,1)S(1)} %bitcast.45), channel_id=1, source_target_pairs={{0,1},{1,2},{2,3},{3,0},{4,5},{5,6},{6,7},{7,4},{8,9},{9,10},{10,1... | collective-permute-start | bytes 1179656 | tf_op jit(solution)/shard_map/ppermute | solution.py:20
  36.6 31.9 %collective-permute-start.2 = (bf16[264,384]{1,0:T(8,128)(2,1)S(1)}, bf16[264,384]{1,0:T(8,128)(2,1)S(1)}, u32[]{:S(2)}, u32[]{:S(2)}) collective-permute-start(bf16[264,384]{1,0:T(8,128)(2,1)S(1)} %get-tuple-element.49), channel_id=1, source_target_pairs={{0,3},{1,0},{2,1},{3,2},{4,7},{5,4},{6,5},{7,6},{8,11},{9,8},{10,9... | collective-permute-start | bytes 608264 | tf_op jit(solution)/shard_map/ppermute | solution.py:20
  58.7 12.4 %collective-permute-start.6 = (bf16[64,1536]{1,0:T(8,128)(2,1)S(1)}, bf16[64,1536]{1,0:T(8,128)(2,1)S(1)}, u32[]{:S(2)}, u32[]{:S(2)}) collective-permute-start(bf16[64,1536]{1,0:T(8,128)(2,1)S(1)} %slice.17), channel_id=1, source_target_pairs={{0,3},{1,0},{2,1},{3,2},{4,7},{5,4},{6,5},{7,6},{8,11},{9,8},{10,9... | collective-permute-start | bytes 589832 | tf_op jit(solution)/shard_map/ppermute | solution.py:20
  62.0 10.9 %collective-permute-start.4 = (bf16[64,1536]{1,0:T(8,128)(2,1)S(1)}, bf16[64,1536]{1,0:T(8,128)(2,1)S(1)}, u32[]{:S(2)}, u32[]{:S(2)}) collective-permute-start(bf16[64,1536]{1,0:T(8,128)(2,1)S(1)} %slice.16), channel_id=1, source_target_pairs={{0,1},{1,2},{2,3},{3,0},{4,5},{5,6},{6,7},{7,4},{8,9},{9,10},{10,1... | collective-permute-start | bytes 589832 | tf_op jit(solution)/shard_map/ppermute | solution.py:20
  62.1 22.4 %collective-permute-start = (bf16[264,384]{1,0:T(8,128)(2,1)S(1)}, bf16[264,384]{1,0:T(8,128)(2,1)S(1)}, u32[]{:S(2)}, u32[]{:S(2)}) collective-permute-start(bf16[264,384]{1,0:T(8,128)(2,1)S(1)} %get-tuple-element.51), channel_id=1, source_target_pairs={{0,1},{1,2},{2,3},{3,0},{4,5},{5,6},{6,7},{7,4},{8,9},{9,10},{10,1... | collective-permute-start | bytes 608264 | tf_op jit(solution)/shard_map/ppermute | solution.py:20
  65.1 19.4 %collective-permute-start.1 = (bf16[264,384]{1,0:T(8,128)(2,1)S(1)}, bf16[264,384]{1,0:T(8,128)(2,1)S(1)}, u32[]{:S(2)}, u32[]{:S(2)}) collective-permute-start(bf16[264,384]{1,0:T(8,128)(2,1)S(1)} %get-tuple-element.52), channel_id=1, source_target_pairs={{0,2},{1,3},{2,0},{3,1},{4,6},{5,7},{6,4},{7,5},{8,10},{9,11},{10,... | collective-permute-start | bytes 608264 | tf_op jit(solution)/shard_map/ppermute | solution.py:20
  68.5 21.9 %collective-permute-start.9 = (bf16[256,384]{1,0:T(8,128)(2,1)S(1)}, bf16[256,384]{1,0:T(8,128)(2,1)S(1)}, u32[]{:S(2)}, u32[]{:S(2)}) collective-permute-start(bf16[256,384]{1,0:T(8,128)(2,1)S(1)} %get-tuple-element.39), channel_id=1, source_target_pairs={{0,3},{1,0},{2,1},{3,2},{4,7},{5,4},{6,5},{7,6},{8,11},{9,8},{10,9... | collective-permute-start | bytes 589832 | tf_op jit(solution)/shard_map/ppermute | solution.py:20
  71.1 19.4 %collective-permute-start.7 = (bf16[256,384]{1,0:T(8,128)(2,1)S(1)}, bf16[256,384]{1,0:T(8,128)(2,1)S(1)}, u32[]{:S(2)}, u32[]{:S(2)}) collective-permute-start(bf16[256,384]{1,0:T(8,128)(2,1)S(1)} %get-tuple-element.40), channel_id=1, source_target_pairs={{0,1},{1,2},{2,3},{3,0},{4,5},{5,6},{6,7},{7,4},{8,9},{9,10},{10,1... | collective-permute-start | bytes 589832 | tf_op jit(solution)/shard_map/ppermute | solution.py:20
  72.9 21.6 %collective-permute-start.8 = (bf16[256,384]{1,0:T(8,128)(2,1)S(1)}, bf16[256,384]{1,0:T(8,128)(2,1)S(1)}, u32[]{:S(2)}, u32[]{:S(2)}) collective-permute-start(bf16[256,384]{1,0:T(8,128)(2,1)S(1)} %get-tuple-element.42), channel_id=1, source_target_pairs={{0,2},{1,3},{2,0},{3,1},{4,6},{5,7},{6,4},{7,5},{8,10},{9,11},{10,... | collective-permute-start | bytes 589832 | tf_op jit(solution)/shard_map/ppermute | solution.py:20
  98.9 8.2 %collective-permute-start.10 = (bf16[128,384]{1,0:T(8,128)(2,1)}, bf16[128,384]{1,0:T(8,128)(2,1)S(1)}, u32[]{:S(2)}, u32[]{:S(2)}) collective-permute-start(bf16[128,384]{1,0:T(8,128)(2,1)} %get-tuple-element.23.refs_9_), channel_id=1, source_target_pairs={{0,3},{1,0},{2,1},{3,2},{4,7},{5,4},{6,5},{7,6},{8,11},{9,8},{10,9... | collective-permute-start | bytes 294920 | tf_op jit(solution)/shard_map/ppermute | solution.py:20
  100.4 8.9 %collective-permute-start.11 = (bf16[128,384]{1,0:T(8,128)(2,1)}, bf16[128,384]{1,0:T(8,128)(2,1)S(1)}, u32[]{:S(2)}, u32[]{:S(2)}) collective-permute-start(bf16[128,384]{1,0:T(8,128)(2,1)} %get-tuple-element.24.refs_10_), channel_id=1, source_target_pairs={{0,2},{1,3},{2,0},{3,1},{4,6},{5,7},{6,4},{7,5},{8,10},{9,11},{10,... | collective-permute-start | bytes 294920 | tf_op jit(solution)/shard_map/ppermute | solution.py:20
  124.7 52.2 %collective-permute-start.23 = (bf16[128,1536]{1,0:T(8,128)(2,1)}, bf16[128,1536]{1,0:T(8,128)(2,1)S(1)}, u32[]{:S(2)}, u32[]{:S(2)}) collective-permute-start(bf16[128,1536]{1,0:T(8,128)(2,1)} %get-tuple-element.35.refs_4_), channel_id=1, source_target_pairs={{0,3},{1,0},{2,1},{3,2},{4,7},{5,4},{6,5},{7,6},{8,11},{9,8},{10,9... | collective-permute-start | bytes 1179656 | tf_op jit(solution)/shard_map/ppermute | solution.py:20
  126.0 50.9 %collective-permute-start.22 = (bf16[128,1536]{1,0:T(8,128)(2,1)}, bf16[128,1536]{1,0:T(8,128)(2,1)S(1)}, u32[]{:S(2)}, u32[]{:S(2)}) collective-permute-start(bf16[128,1536]{1,0:T(8,128)(2,1)} %get-tuple-element.35.refs_4_), channel_id=1, source_target_pairs={{0,2},{1,3},{2,0},{3,1},{4,6},{5,7},{6,4},{7,5},{8,10},{9,11},{10,... | collective-permute-start | bytes 1179656 | tf_op jit(solution)/shard_map/ppermute | solution.py:20
  130.4 46.5 %collective-permute-start.21 = (bf16[128,1536]{1,0:T(8,128)(2,1)}, bf16[128,1536]{1,0:T(8,128)(2,1)S(1)}, u32[]{:S(2)}, u32[]{:S(2)}) collective-permute-start(bf16[128,1536]{1,0:T(8,128)(2,1)} %get-tuple-element.35.refs_4_), channel_id=1, source_target_pairs={{0,1},{1,2},{2,3},{3,0},{4,5},{5,6},{6,7},{7,4},{8,9},{9,10},{10,1... | collective-permute-start | bytes 1179656 | tf_op jit(solution)/shard_map/ppermute | solution.py:20
  131.2 28.4 %collective-permute-start.16 = (bf16[136,384]{1,0:T(8,128)(2,1)S(1)}, bf16[136,384]{1,0:T(8,128)(2,1)S(1)}, u32[]{:S(2)}, u32[]{:S(2)}) collective-permute-start(bf16[136,384]{1,0:T(8,128)(2,1)S(1)} %get-tuple-element.29), channel_id=1, source_target_pairs={{0,1},{1,2},{2,3},{3,0},{4,5},{5,6},{6,7},{7,4},{8,9},{9,10},{10,1... | collective-permute-start | bytes 313352 | tf_op jit(solution)/shard_map/ppermute | solution.py:20
  131.6 28.3 %collective-permute-start.17 = (bf16[136,384]{1,0:T(8,128)(2,1)S(1)}, bf16[136,384]{1,0:T(8,128)(2,1)S(1)}, u32[]{:S(2)}, u32[]{:S(2)}) collective-permute-start(bf16[136,384]{1,0:T(8,128)(2,1)S(1)} %get-tuple-element.30), channel_id=1, source_target_pairs={{0,2},{1,3},{2,0},{3,1},{4,6},{5,7},{6,4},{7,5},{8,10},{9,11},{10,... | collective-permute-start | bytes 313352 | tf_op jit(solution)/shard_map/ppermute | solution.py:20
  159.6 11.8 %collective-permute-start.18 = (bf16[136,384]{1,0:T(8,128)(2,1)S(1)}, bf16[136,384]{1,0:T(8,128)(2,1)S(1)}, u32[]{:S(2)}, u32[]{:S(2)}) collective-permute-start(bf16[136,384]{1,0:T(8,128)(2,1)S(1)} %get-tuple-element.31), channel_id=1, source_target_pairs={{0,3},{1,0},{2,1},{3,2},{4,7},{5,4},{6,5},{7,6},{8,11},{9,8},{10,9... | collective-permute-start | bytes 313352 | tf_op jit(solution)/shard_map/ppermute | solution.py:20
  187.4 35.9 %all-to-all-start.1 = ((bf16[32,24,768]{2,1,0:T(8,128)(2,1)}), bf16[32,24,768]{2,1,0:T(8,128)(2,1)}, u32[]{:S(2)}, u32[]{:S(2)}) async-start(bf16[32,24,768]{2,1,0:T(8,128)(2,1)} %add_convert_fusion), calls=%async_computation.1 | async-start | bytes 2359296 | tf_op jit(solution)/shard_map/all_to_all | solution.py:432
  223.4 23.8 %all-to-all-start = ((bf16[32,24,768]{2,1,0:T(8,128)(2,1)}), bf16[32,24,768]{2,1,0:T(8,128)(2,1)S(1)}, u32[]{:S(2)}, u32[]{:S(2)}) async-start(bf16[32,24,768]{2,1,0:T(8,128)(2,1)} %bitcast.17), calls=%async_computation | async-start | bytes 2359296 | tf_op jit(solution)/shard_map/all_to_all | solution.py:432
  (35 other events, 481.2 us)
Sparse Core Ops, SparseCore 0:
  31.7 71.8 all-gather.1
